TPU v7x, 32 devices: a whole 2x2x4 slice. The times are simulated.
32 devices in a mesh: gx: 4 (over z), gy: 2 (over y), gz: 4 (over x, core).
Axes of the slice: x: 2, y: 2, z: 4, core: 2. Of those that a mesh axis runs over, the one named last changes fastest.
Arguments:
- density: float32 [32, 16, 512], P('gx', 'gy', 'gz'), may hold values from 0.5 to 2
- base_velocity: float32 [3, 32, 16, 512], P(None, 'gx', 'gy', 'gz'), may hold values from -0.4 to 0.4
- cells: int32 [3, 8192], P(None, ('gx', 'gy', 'gz')), may hold values from 0 to 511, as said below
- offsets: float32 [3, 8192], P(None, ('gx', 'gy', 'gz')), may hold values from 0 to 1
- target: float32 [3, 8192], P(None, ('gx', 'gy', 'gz')), may hold values from -0.4 to 0.4
- stiffness: float32 [8192], P(('gx', 'gy', 'gz')), may hold values from 0.01 to 0.1
- counts: int32 [32], P(('gx', 'gy', 'gz')), may hold values from 1 to 256, as said below
Outputs:
- forces: float32 [3, 8192], P(None, ('gx', 'gy', 'gz'))
Inputs may be any that keep to these rules, and one draw needn't show every extreme that they name: `cells`: each marker's cell lies inside the lattice block of the device that holds its slot. `counts`: some device holds exactly 256 live markers in every draw.
All inputs are finite; a program needn't handle non-finite values.
Results may differ from a plain program's by a relative error of at most 0.0001.
Values sent between devices are 32-bit elements; how exact they have to be, the bound alone decides.
A program may use at most 64 MiB of HBM per device.

v0:
```python
import functools
import itertools

import jax
import jax.numpy as jnp
from jax import lax
from jax.experimental import pallas as pl
from jax.experimental.pallas import tpu as pltpu
from jax.sharding import PartitionSpec as P

ITERS = 3
MOST_DIRECT = 64
LOW, HIGH = 2, 3
MESH_ID = pl.DeviceIdType.MESH
AXES = ("gx", "gy", "gz")


def round_up(value, multiple):
    return -(-value // multiple) * multiple


def axis_groups(count):
    groups = {}
    for shift in (0, -1, 1):
        groups.setdefault(shift % count, []).append(shift)
    return list(groups.items())


def span(shifts, size):
    if shifts == [0]:
        return 1, size + 3
    if shifts == [-1]:
        return 0, 4
    if shifts == [1]:
        return size + 1, 4
    return 0, size + 5


def weights(fraction):
    root = jnp.sqrt(1.0 + 4.0 * fraction - 4.0 * fraction * fraction)
    near, far = 3.0 - 2.0 * fraction, 1.0 + 2.0 * fraction
    return ((near - root) / 8.0, (near + root) / 8.0, (far + root) / 8.0, (far - root) / 8.0)


def table(cell, four, shifts, size, first, rows):
    place = lax.broadcasted_iota(jnp.int32, (rows, cell.shape[1]), 0).astype(jnp.float32) + first
    total = None
    for shift in shifts:
        apart = place - (cell + (1.0 + shift * size))
        part = jnp.where(apart == 3.0, four[3], 0.0)
        for number in (2, 1, 0):
            part = jnp.where(apart == float(number), four[number], part)
        total = part if total is None else total + part
    return total


def split(value):
    high = value.astype(jnp.bfloat16)
    return high, (value - high.astype(jnp.float32)).astype(jnp.bfloat16)


def dot_nt(a, b):
    return lax.dot_general(a, b, (((1,), (1,)), ((), ())), preferred_element_type=jnp.float32)


def dot_nn(a, b):
    return lax.dot_general(a, b, (((1,), (0,)), ((), ())), preferred_element_type=jnp.float32)


def kernel(
    counts, sizes, block, marks, aux, out, fields, xbuf, ybuf, zpack, zbuf, nbuf, fbuf, rbuf, dbuf, txy, thi, tlo, whi, wlo, grid,
    nsend, nrecv, rsend, rrecv, dsend, drecv, hsend, hrecv,
):
    size_x, size_y, size_z = sizes
    cap = marks.shape[1]
    rows_y, lanes = fields.shape[2], fields.shape[3]
    assert 8 * (size_x + 5) <= size_z == lanes - size_z
    wide_x = size_x + 5
    groups = [axis_groups(count) for count in counts]
    slots = list(itertools.product(*[[offset for offset, _ in group] for group in groups]))
    me = [lax.axis_index(name) for name in AXES]
    sent = []

    def device(offset):
        return tuple(lax.rem(m + o, n) for m, o, n in zip(me, offset, counts))

    def negated(offset):
        return tuple((-o) % n for o, n in zip(offset, counts))

    peers = {slot for slot in slots if any(slot)}
    for axis, count in enumerate(counts):
        for step in range(1, count):
            peers.add(tuple(step if a == axis else 0 for a in range(3)))
    everyone = [o for o in itertools.product(*[range(n) for n in counts]) if any(o)]
    direct = len(everyone) < MOST_DIRECT
    peers = everyone if direct else sorted(peers)
    barrier = pltpu.get_barrier_semaphore()
    for peer in peers:
        pl.semaphore_signal(barrier, inc=1, device_id=device(peer), device_id_type=MESH_ID)
    pl.semaphore_wait(barrier, len(peers))

    def neighbour_copy(turn, number):
        return pltpu.make_async_remote_copy(
            src_ref=fbuf.at[turn - 1, 0] if turn else nbuf.at[0],
            dst_ref=fbuf.at[turn - 1, number] if turn else nbuf.at[number],
            send_sem=nsend.at[turn, number - 1],
            recv_sem=nrecv.at[turn, number - 1],
            device_id=device(negated(slots[number])),
            device_id_type=MESH_ID,
        )

    def send_round(turn):
        for number in sorted(range(1, len(slots)), key=lambda k: (slots[k][0] == 0, k)):
            copy = neighbour_copy(turn, number)
            copy.start()
            sent.append(copy)

    def wait_round(turn, off_x):
        for number in range(1, len(slots)):
            if slots[number][0] == off_x:
                neighbour_copy(turn, number).wait_recv()

    def sum_copy(turn, stage, step):
        axis = 2 - stage
        offset = tuple((-step) % counts[axis] if a == axis else 0 for a in range(3))
        return pltpu.make_async_remote_copy(
            src_ref=rbuf.at[turn, stage, 0],
            dst_ref=rbuf.at[turn, stage, step],
            send_sem=rsend.at[turn, stage, step - 1],
            recv_sem=rrecv.at[turn, stage, step - 1],
            device_id=device(offset),
            device_id_type=MESH_ID,
        )

    def send_sum(turn, stage, value):
        rbuf[turn, stage, 0] = value
        for step in range(1, counts[2 - stage]):
            copy = sum_copy(turn, stage, step)
            copy.start()
            sent.append(copy)

    def wait_sum(turn, stage):
        for step in range(1, counts[2 - stage]):
            sum_copy(turn, stage, step).wait_recv()
        total = rbuf[turn, stage, 0]
        for step in range(1, counts[2 - stage]):
            total = total + rbuf[turn, stage, step]
        return total

    def put(turn, vector):
        for c in range(3):
            for part in range(cap // 128):
                fbuf[turn - 1, 0, pl.ds(c * (cap // 128) + part, 1), :] = vector[
                    c : c + 1, part * 128 : part * 128 + 128
                ]

    def taken(turn, number, c):
        each = cap // 128
        return jnp.concatenate(
            [fbuf[turn - 1, number, pl.ds(c * each + part, 1), :] for part in range(each)], axis=1
        )

    def direct_copy(number):
        return pltpu.make_async_remote_copy(
            src_ref=dbuf.at[0],
            dst_ref=dbuf.at[number + 1],
            send_sem=dsend.at[number],
            recv_sem=drecv.at[number],
            device_id=device(negated(everyone[number])),
            device_id_type=MESH_ID,
        )

    def sum_directly(value):
        dbuf[0] = value
        for number in range(len(everyone)):
            copy = direct_copy(number)
            copy.start()
            sent.append(copy)
        for number in range(len(everyone)):
            direct_copy(number).wait_recv()
        return jnp.sum(dbuf[...], axis=0)

    offs_y = sorted({1 % counts[1], (-1) % counts[1]})
    offs_z = sorted({1 % counts[2], (-1) % counts[2]})

    def halo_copy(number, source, target, offset):
        return pltpu.make_async_remote_copy(
            src_ref=source,
            dst_ref=target,
            send_sem=hsend.at[number],
            recv_sem=hrecv.at[number],
            device_id=device(negated(offset)),
            device_id_type=MESH_ID,
        )

    def go(copies):
        for copy in copies:
            copy.start()
            sent.append(copy)

    low, high = pl.ds(0, LOW), pl.ds(LOW, HIGH)
    along_x = [
        halo_copy(0, block.at[:, pl.ds(size_x - LOW, LOW)], xbuf.at[:, low], (counts[0] - 1, 0, 0)),
        halo_copy(1, block.at[:, pl.ds(0, HIGH)], xbuf.at[:, high], (1, 0, 0)),
    ]
    along_y, relayed_y = [], []
    for k, off in enumerate(offs_y):
        here = (0, off, 0)
        along_y.append(halo_copy(2 + k, block, ybuf.at[k, :, pl.ds(LOW, size_x)], here))
        relayed_y.append(halo_copy(4 + k, xbuf.at[:, low], ybuf.at[k, :, low], here))
        relayed_y.append(
            halo_copy(6 + k, xbuf.at[:, high], ybuf.at[k, :, pl.ds(LOW + size_x, HIGH)], here)
        )
    along_z = [halo_copy(8 + k, zpack, zbuf.at[k], (0, 0, off)) for k, off in enumerate(offs_z)]

    def widen():
        for copy in along_y + relayed_y:
            copy.wait_recv()
        below = ybuf.at[offs_y.index((-1) % counts[1])]
        above = ybuf.at[offs_y.index(1 % counts[1])]
        lane = lax.broadcasted_iota(jnp.int32, (4, rows_y, size_z), 2)
        zero = jnp.zeros((4, rows_y - size_y - LOW - HIGH, size_z), jnp.float32)
        packed = jnp.zeros((4, rows_y, size_z), jnp.float32)
        for plane in range(wide_x):
            if plane < LOW:
                own = xbuf[:, plane]
            elif plane < LOW + size_x:
                own = block[:, plane - LOW]
            else:
                own = xbuf[:, plane - size_x]
            tall = jnp.concatenate(
                [below[:, plane][:, size_y - LOW :], own, above[:, plane][:, :HIGH], zero], axis=1
            )
            fields[:, plane, :, pl.ds(0, size_z)] = tall
            ends = jnp.where(lane < HIGH, tall, pltpu.roll(tall, LOW + HIGH, 2))
            at = 8 * plane
            inside = (lane >= at) & (lane < at + LOW + HIGH)
            packed = jnp.where(inside, pltpu.roll(ends, at, 2) if at else ends, packed)
        zpack[...] = packed
        go(along_z)
        for copy in along_z:
            copy.wait_recv()
        before = zbuf[offs_z.index((-1) % counts[2])]
        after = zbuf[offs_z.index(1 % counts[2])]
        for plane in range(wide_x):
            at = 8 * plane
            tall = pltpu.roll(fields[:, plane, :, pl.ds(0, size_z)], LOW, 2)
            first = pltpu.roll(before, (-(at + HIGH)) % size_z, 2)
            last = pltpu.roll(after, (LOW - at) % size_z, 2)
            fields[:, plane, :, pl.ds(0, size_z)] = jnp.where(lane < LOW, first, tall)
            tail = jnp.where(lane < LOW, tall, jnp.where(lane < LOW + HIGH, last, 0.0))
            fields[:, plane, :, pl.ds(size_z, lanes - size_z)] = tail

    go(along_x + along_y)
    nbuf[0] = marks[...]
    send_round(0)

    def build(xi, yi, zi):
        number = slots.index((groups[0][xi][0], groups[1][yi][0], groups[2][zi][0]))
        info = nbuf[number]
        cells = [info[k : k + 1] for k in range(3)]
        fours = [weights(info[k + 3 : k + 4]) for k in range(3)]
        block = (yi * len(groups[2]) + zi) * cap
        start, planes = span(groups[0][xi][1], size_x)
        first = start // 8 * 8
        tall = round_up(start + planes - first, 8)
        tab_x = table(cells[0], fours[0], groups[0][xi][1], size_x, float(first), tall)
        tab_y = table(cells[1], fours[1], groups[1][yi][1], size_y, 0.0, rows_y)
        for plane in range(planes):
            at = start - first + plane
            txy[xi, pl.ds(plane * rows_y, rows_y), pl.ds(block, cap)] = tab_x[at : at + 1] * tab_y
        shifts = groups[2][zi][1]
        start, planes = span(shifts, size_z)
        first = start // 16 * 16
        tall = round_up(start + planes - first, 16)
        tab_z = table(cells[2], fours[2], shifts, size_z, float(first), tall)
        high, low = split(tab_z)
        for ref, part in ((thi, high), (tlo, low)):
            if first:
                ref[xi, pl.ds(0, first), pl.ds(block, cap)] = jnp.zeros((first, cap), jnp.bfloat16)
            ref[xi, pl.ds(first, tall), pl.ds(block, cap)] = part
            rest = lanes - first - tall
            if rest:
                ref[xi, pl.ds(first + tall, rest), pl.ds(block, cap)] = jnp.zeros(
                    (rest, cap), jnp.bfloat16
                )

    start_own, planes_own = span(groups[0][0][1], size_x)

    def interpolate(field):
        rows = planes_own * rows_y
        high, low = split(field.reshape(3 * rows, lanes))
        z_high, z_low = thi[0, :, pl.ds(0, cap)], tlo[0, :, pl.ds(0, cap)]
        part = dot_nn(high, z_high) + dot_nn(low, z_high) + dot_nn(high, z_low)
        plane = txy[0, pl.ds(0, rows), pl.ds(0, cap)]
        return jnp.concatenate(
            [
                jnp.sum(part[c * rows : (c + 1) * rows] * plane, axis=0, keepdims=True)
                for c in range(3)
            ],
            axis=0,
        )

    def spread(turn):
        for xi, (off_x, shifts) in enumerate(groups[0]):
            start, planes = span(shifts, size_x)
            rows = planes * rows_y
            wait_round(turn, off_x)
            for yi, (off_y, _) in enumerate(groups[1]):
                for zi, (off_z, _) in enumerate(groups[2]):
                    number = slots.index((off_x, off_y, off_z))
                    block = (yi * len(groups[2]) + zi) * cap
                    plane = txy[xi, pl.ds(0, rows), pl.ds(block, cap)]
                    for c in range(3):
                        high, low = split(plane * taken(turn, number, c))
                        whi[pl.ds(c * rows, rows), pl.ds(block, cap)] = high
                        wlo[pl.ds(c * rows, rows), pl.ds(block, cap)] = low
            high, low = whi[pl.ds(0, 3 * rows), :], wlo[pl.ds(0, 3 * rows), :]
            part = dot_nt(high, thi[xi]) + dot_nt(low, thi[xi]) + dot_nt(high, tlo[xi])
            part = part.reshape(3, planes, rows_y, lanes)
            if xi == 0:
                if start > 0:
                    grid[:, pl.ds(0, start)] = jnp.zeros((3, start, rows_y, lanes), jnp.float32)
                rest = wide_x - start - planes
                if rest > 0:
                    grid[:, pl.ds(start + planes, rest)] = jnp.zeros(
                        (3, rest, rows_y, lanes), jnp.float32
                    )
                grid[:, pl.ds(start, planes)] = part
            else:
                grid[:, pl.ds(start, planes)] += part

    def shifted(value, by, axis):
        return pltpu.roll(value, by % value.shape[axis], axis)

    def both(value, axis):
        return shifted(value, -1, axis), shifted(value, 1, axis)

    def add(value, axis):
        up, down = both(value, axis)
        return up + down

    def sub(value, axis):
        up, down = both(value, axis)
        return up - down

    def respond():
        scale = fields[3]
        mx, my, mz = (scale * grid[c] for c in range(3))
        slope_y, slope_z = sub(my, 1), sub(mz, 2)
        sum_x = 2.0 * mx + add(mx, 1) + add(mx, 2)
        slope = slope_y + slope_z
        px = sum_x[2:] + sum_x[:-2] + slope[2:] - slope[:-2]
        slope_x = mx[2:] - mx[:-2]
        sum_y = (2.0 * my + add(my, 2))[1:-1] + my[2:] + my[:-2]
        py = add(sum_y, 1) + sub(slope_x + slope_z[1:-1], 1)
        sum_z = (2.0 * mz + add(mz, 1))[1:-1] + mz[2:] + mz[:-2]
        pz = add(sum_z, 2) + sub(slope_x + slope_y[1:-1], 2)
        half = scale[1:-1] * 0.5
        return jnp.stack(
            [half * (m[1:-1] + p * (1.0 / 12.0)) for m, p in ((mx, px), (my, py), (mz, pz))]
        )

    target, stiffness, live = aux[pl.ds(0, 3), :], aux[pl.ds(3, 1), :], aux[pl.ds(4, 1), :]

    def apply(turn, vector, summing=None):
        spread(turn)
        if summing is not None:
            send_sum(summing, 1, wait_sum(summing, 0))
        field = respond()
        if summing is not None:
            send_sum(summing, 2, wait_sum(summing, 1))
        return live * (interpolate(field) + stiffness * vector)

    def partial_sums(residual, image):
        folded = []
        for other in (residual, image):
            row = jnp.sum(residual * other, axis=0, keepdims=True)
            total = row[:, :128]
            for at in range(128, cap, 128):
                total = total + row[:, at : at + 128]
            folded.append(total)
        return jnp.concatenate(folded, axis=0)

    def totals(tile):
        return (
            jnp.sum(tile[0:1], axis=1, keepdims=True),
            jnp.sum(tile[1:2], axis=1, keepdims=True),
        )

    build(0, 0, 0)
    for copy in along_x:
        copy.wait_recv()
    go(relayed_y)
    for off_x, _ in groups[0]:
        wait_round(0, off_x)
    for xi, yi, zi in itertools.product(*[range(len(group)) for group in groups]):
        if (xi, yi, zi) != (0, 0, 0):
            build(xi, yi, zi)
    widen()
    residual = live * (target - interpolate(fields[pl.ds(0, 3), pl.ds(1, size_x + 3)]))
    put(1, residual)
    send_round(1)

    image = apply(1, residual)
    direction, along, along_image = residual, image, None
    answer = None
    norm_before = alpha = None
    for step in range(ITERS):
        sums = partial_sums(residual, image)
        if step + 1 < ITERS or not direct:
            send_sum(step, 0, sums)
        if step + 1 < ITERS:
            put(step + 2, image)
            send_round(step + 2)
            ahead = apply(step + 2, image, step)
            norm, product = totals(wait_sum(step, 2))
        elif direct:
            norm, product = totals(sum_directly(sums))
        else:
            send_sum(step, 1, wait_sum(step, 0))
            send_sum(step, 2, wait_sum(step, 1))
            norm, product = totals(wait_sum(step, 2))
        if step == 0:
            alpha = norm / product
            along_image = ahead
        else:
            ratio = norm / norm_before
            alpha = norm / (product - ratio * norm / alpha)
            direction = residual + ratio * direction
            if step + 1 < ITERS:
                along = image + ratio * along
                along_image = ahead + ratio * along_image
        answer = alpha * direction if answer is None else answer + alpha * direction
        norm_before = norm
        if step + 1 < ITERS:
            residual = residual - alpha * along
            image = image - alpha * along_image
    out[...] = answer
    for copy in sent:
        copy.wait_send()


def body(mesh_counts, density, base_velocity, cells, offsets, target, stiffness, counts):
    sizes = density.shape
    size_x, size_y, size_z = sizes
    cap = cells.shape[1]
    rows_y, lanes = round_up(size_y + 5, 16), round_up(size_z + 5, 128)
    anchor = jnp.stack([lax.axis_index(name) * size for name, size in zip(AXES, sizes)])
    local = (cells - anchor[:, None]).astype(jnp.float32)
    marks = jnp.concatenate([local, offsets, jnp.zeros((2, cap), jnp.float32)], axis=0)
    live = (jnp.arange(cap, dtype=jnp.int32) < counts[0]).astype(jnp.float32)
    aux = jnp.concatenate(
        [target, stiffness[None], live[None], jnp.zeros((3, cap), jnp.float32)], axis=0
    )
    stacked = jnp.concatenate([base_velocity, lax.rsqrt(density)[None]], axis=0)
    groups = [axis_groups(count) for count in mesh_counts]
    number = len(groups[0]) * len(groups[1]) * len(groups[2])
    width = len(groups[1]) * len(groups[2]) * cap
    tallest = max(span(shifts, size_x)[1] for _, shifts in groups[0])
    longest = max(mesh_counts)
    turns = ITERS + 1
    devices = mesh_counts[0] * mesh_counts[1] * mesh_counts[2]
    most = devices if devices <= MOST_DIRECT else 1
    return pl.pallas_call(
        functools.partial(kernel, mesh_counts, sizes),
        out_shape=jax.ShapeDtypeStruct((3, cap), jnp.float32),
        in_specs=[pl.BlockSpec(memory_space=pltpu.VMEM)] * 3,
        out_specs=pl.BlockSpec(memory_space=pltpu.VMEM),
        scratch_shapes=[
            pltpu.VMEM((4, size_x + 5, rows_y, lanes), jnp.float32),
            pltpu.VMEM((4, LOW + HIGH, size_y, size_z), jnp.float32),
            pltpu.VMEM((2, 4, size_x + 5, size_y, size_z), jnp.float32),
            pltpu.VMEM((4, rows_y, size_z), jnp.float32),
            pltpu.VMEM((2, 4, rows_y, size_z), jnp.float32),
            pltpu.VMEM((number, 8, cap), jnp.float32),
            pltpu.VMEM((ITERS, number, 3 * (cap // 128), 128), jnp.float32),
            pltpu.VMEM((ITERS, 3, longest, 2, 128), jnp.float32),
            pltpu.VMEM((most, 2, 128), jnp.float32),
            pltpu.VMEM((len(groups[0]), tallest * rows_y, width), jnp.float32),
            pltpu.VMEM((len(groups[0]), lanes, width), jnp.bfloat16),
            pltpu.VMEM((len(groups[0]), lanes, width), jnp.bfloat16),
            pltpu.VMEM((3 * tallest * rows_y, width), jnp.bfloat16),
            pltpu.VMEM((3 * tallest * rows_y, width), jnp.bfloat16),
            pltpu.VMEM((3, size_x + 5, rows_y, lanes), jnp.float32),
            pltpu.SemaphoreType.DMA((turns, number - 1)),
            pltpu.SemaphoreType.DMA((turns, number - 1)),
            pltpu.SemaphoreType.DMA((ITERS, 3, longest - 1)),
            pltpu.SemaphoreType.DMA((ITERS, 3, longest - 1)),
            pltpu.SemaphoreType.DMA((most,)),
            pltpu.SemaphoreType.DMA((most,)),
            pltpu.SemaphoreType.DMA((10,)),
            pltpu.SemaphoreType.DMA((10,)),
        ],
        compiler_params=pltpu.CompilerParams(
            collective_id=0, has_side_effects=True, vmem_limit_bytes=60 * 1024 * 1024
        ),
    )(stacked, marks, aux)


def solution(mesh):
    return jax.shard_map(
        functools.partial(body, tuple(mesh.shape[name] for name in AXES)),
        mesh=mesh,
        in_specs=(
            P("gx", "gy", "gz"),
            P(None, "gx", "gy", "gz"),
            P(None, ("gx", "gy", "gz")),
            P(None, ("gx", "gy", "gz")),
            P(None, ("gx", "gy", "gz")),
            P(("gx", "gy", "gz")),
            P(("gx", "gy", "gz")),
        ),
        out_specs=P(None, ("gx", "gy", "gz")),
        check_vma=False,
    )
```

profile of v0, /device:TPU:0, one launch (start us, length us, event | category | flops | bytes accessed | tf_op | source)
XLA Modules:
  0.0 73.3 jit_solution(2110244708088033304)
XLA Ops:
  0.0 0.8 %rsqrt_bitcast_fusion = f32[1,8,8,128]{3,2,1,0:T(8,128)S(1)} fusion(f32[8,8,128]{2,1,0:T(8,128)} %param.7), kind=kLoop, calls=%fused_computation.1 | loop fusion | bytes 65536 | tf_op jit(solution)/shard_map/broadcast_in_dim | solution.py:456
  0.8 1.6 %pad_maximum_fusion.block = f32[4,8,8,128]{3,2,1,0:T(8,128)} fusion(f32[1,8,8,128]{3,2,1,0:T(8,128)S(1)} %rsqrt_bitcast_fusion, f32[3,8,8,128]{3,2,1,0:T(8,128)} %param.8), kind=kLoop, calls=%fused_computation | loop fusion | flops 32768 | bytes 262144 | tf_op jit(solution)/shard_map/concatenate | solution.py:456
  2.3 0.0 copy-start
  2.3 0.1 pad_add_fusion
  2.4 0.6 copy-done
  3.0 0.1 subtract_convert_fusion
  3.1 0.1 pad.6.clone
  3.2 0.0 copy-start.2
  3.2 0.1 pad.3.clone
  3.2 0.0 copy-start.1
  3.9 0.0 copy-start.3
  3.9 0.0 copy-done.2
  3.9 0.0 copy-done.1
  4.0 0.7 copy-done.3
  4.6 0.7 maximum_maximum_fusion
  5.3 66.7 %shard_map.73 = f32[3,256]{1,0:T(4,128)} custom-call(f32[4,8,8,128]{3,2,1,0:T(8,128)} %pad_maximum_fusion.block, f32[8,256]{1,0:T(8,128)} %get-tuple-element.5.marks, f32[8,256]{1,0:T(8,128)} %get-tuple-element.6.aux), custom_call_target="tpu_custom_call" | custom-call | tf_op jit(solution)/shard_map/pallas_call | solution.py:465
  72.0 1.3 %copy.10 = f32[3,256]{1,0:T(4,128)} copy(f32[3,256]{1,0:T(4,128)} %shard_map.73) | data formatting | bytes 6144
  (3 shorter events, 0.0 us)
Async XLA Ops:
  2.3 0.7 copy-start
  3.2 0.8 %copy-start.2 = (f32[3,256]{1,0:T(4,128)S(1)}, f32[3,256]{1,0:T(4,128)}, u32[]{:S(2)}) copy-start(f32[3,256]{1,0:T(4,128)} %param.11) | copy-start | bytes 9220
  3.2 0.7 copy-start.1
  3.9 0.7 copy-start.3
where the time goes:
time: 73.6 us; the launch traced here: 73.3 us
  Pallas kernels  66.7 us (91%)
  local copies, waits for them, and re-layouts  3.47 us (5%)
  other arithmetic  2.38 us (3%)
    pallas_call x1, Pallas kernels, body(): pl.pallas_call(functools.partial(kernel, mesh_counts, sizes), out_shape=j...  66.7 us
    unnamed x9, local copies, waits for them, and re-layouts  2.55 us
    concatenate x1, other arithmetic, body(): stacked = jnp.concatenate([base_velocity, lax.rsqrt(density)[None]], axis=0)  1.56 us

commit v1 on v0

--- a/solution.py
+++ b/solution.py
@@ -68,11 +68,12 @@
 
 
 def kernel(
-    counts, sizes, block, marks, aux, out, fields, xbuf, ybuf, zpack, zbuf, nbuf, fbuf, rbuf, dbuf, txy, thi, tlo, whi, wlo, grid,
-    nsend, nrecv, rsend, rrecv, dsend, drecv, hsend, hrecv,
+    counts, sizes, density_in, velocity_in, cells_in, offsets_in, target_in, stiffness_in, live_in, out,
+    block, dense, cell, offset, target, stiffness, held, fields, xbuf, ybuf, zpack, zbuf, nbuf, fbuf, rbuf, dbuf, txy, thi, tlo, whi, wlo,
+    grid, lsem, nsend, nrecv, rsend, rrecv, dsend, drecv, hsend, hrecv,
 ):
     size_x, size_y, size_z = sizes
-    cap = marks.shape[1]
+    cap = cell.shape[1]
     rows_y, lanes = fields.shape[2], fields.shape[3]
     assert 8 * (size_x + 5) <= size_z == lanes - size_z
     wide_x = size_x + 5
@@ -94,9 +95,27 @@
     everyone = [o for o in itertools.product(*[range(n) for n in counts]) if any(o)]
     direct = len(everyone) < MOST_DIRECT
     peers = everyone if direct else sorted(peers)
+    loads = [
+        pltpu.make_async_copy(source, target_ref, lsem.at[number])
+        for number, (source, target_ref) in enumerate((
+            (density_in, dense), (velocity_in, block.at[pl.ds(0, 3)]), (cells_in, cell), (offsets_in, offset),
+            (target_in, target), (stiffness_in, stiffness), (live_in, held),
+        ))
+    ]
     barrier = pltpu.get_barrier_semaphore()
     for peer in peers:
         pl.semaphore_signal(barrier, inc=1, device_id=device(peer), device_id_type=MESH_ID)
+    for load in loads:
+        load.start()
+    for load in loads:
+        load.wait()
+    block[3] = lax.rsqrt(dense[...])
+    corner = [m * size for m, size in zip(me, sizes)]
+    for k in range(3):
+        nbuf[0, pl.ds(k, 1), :] = (cell[pl.ds(k, 1), :] - corner[k]).astype(jnp.float32)
+    nbuf[0, pl.ds(3, 3), :] = offset[...]
+    nbuf[0, pl.ds(6, 2), :] = jnp.zeros((2, cap), jnp.float32)
+    live = (lax.broadcasted_iota(jnp.int32, (1, cap), 1) < held[0]).astype(jnp.float32)
     pl.semaphore_wait(barrier, len(peers))
 
     def neighbour_copy(turn, number):
@@ -160,25 +179,27 @@
             [fbuf[turn - 1, number, pl.ds(c * each + part, 1), :] for part in range(each)], axis=1
         )
 
-    def direct_copy(number):
+    def direct_copy(step, number):
         return pltpu.make_async_remote_copy(
-            src_ref=dbuf.at[0],
-            dst_ref=dbuf.at[number + 1],
-            send_sem=dsend.at[number],
-            recv_sem=drecv.at[number],
+            src_ref=dbuf.at[step, 0],
+            dst_ref=dbuf.at[step, number + 1],
+            send_sem=dsend.at[step, number],
+            recv_sem=drecv.at[step, number],
             device_id=device(negated(everyone[number])),
             device_id_type=MESH_ID,
         )
 
-    def sum_directly(value):
-        dbuf[0] = value
+    def send_directly(step, value):
+        dbuf[step, 0] = value
         for number in range(len(everyone)):
-            copy = direct_copy(number)
+            copy = direct_copy(step, number)
             copy.start()
             sent.append(copy)
+
+    def wait_directly(step):
         for number in range(len(everyone)):
-            direct_copy(number).wait_recv()
-        return jnp.sum(dbuf[...], axis=0)
+            direct_copy(step, number).wait_recv()
+        return jnp.sum(dbuf[step], axis=0)
 
     offs_y = sorted({1 % counts[1], (-1) % counts[1]})
     offs_z = sorted({1 % counts[2], (-1) % counts[2]})
@@ -252,7 +273,6 @@
             fields[:, plane, :, pl.ds(size_z, lanes - size_z)] = tail
 
     go(along_x + along_y)
-    nbuf[0] = marks[...]
     send_round(0)
 
     def build(xi, yi, zi):
@@ -361,8 +381,6 @@
             [half * (m[1:-1] + p * (1.0 / 12.0)) for m, p in ((mx, px), (my, py), (mz, pz))]
         )
 
-    target, stiffness, live = aux[pl.ds(0, 3), :], aux[pl.ds(3, 1), :], aux[pl.ds(4, 1), :]
-
     def apply(turn, vector, summing=None):
         spread(turn)
         if summing is not None:
@@ -370,7 +388,7 @@
         field = respond()
         if summing is not None:
             send_sum(summing, 2, wait_sum(summing, 1))
-        return live * (interpolate(field) + stiffness * vector)
+        return live * (interpolate(field) + stiffness[...] * vector)
 
     def partial_sums(residual, image):
         folded = []
@@ -398,7 +416,7 @@
         if (xi, yi, zi) != (0, 0, 0):
             build(xi, yi, zi)
     widen()
-    residual = live * (target - interpolate(fields[pl.ds(0, 3), pl.ds(1, size_x + 3)]))
+    residual = live * (target[...] - interpolate(fields[pl.ds(0, 3), pl.ds(1, size_x + 3)]))
     put(1, residual)
     send_round(1)
 
@@ -408,16 +426,20 @@
     norm_before = alpha = None
     for step in range(ITERS):
         sums = partial_sums(residual, image)
-        if step + 1 < ITERS or not direct:
-            send_sum(step, 0, sums)
         if step + 1 < ITERS:
             put(step + 2, image)
             send_round(step + 2)
+        if direct:
+            send_directly(step, sums)
+            if step + 1 < ITERS:
+                ahead = apply(step + 2, image)
+            norm, product = totals(wait_directly(step))
+        elif step + 1 < ITERS:
+            send_sum(step, 0, sums)
             ahead = apply(step + 2, image, step)
             norm, product = totals(wait_sum(step, 2))
-        elif direct:
-            norm, product = totals(sum_directly(sums))
         else:
+            send_sum(step, 0, sums)
             send_sum(step, 1, wait_sum(step, 0))
             send_sum(step, 2, wait_sum(step, 1))
             norm, product = totals(wait_sum(step, 2))
@@ -446,14 +468,6 @@
     size_x, size_y, size_z = sizes
     cap = cells.shape[1]
     rows_y, lanes = round_up(size_y + 5, 16), round_up(size_z + 5, 128)
-    anchor = jnp.stack([lax.axis_index(name) * size for name, size in zip(AXES, sizes)])
-    local = (cells - anchor[:, None]).astype(jnp.float32)
-    marks = jnp.concatenate([local, offsets, jnp.zeros((2, cap), jnp.float32)], axis=0)
-    live = (jnp.arange(cap, dtype=jnp.int32) < counts[0]).astype(jnp.float32)
-    aux = jnp.concatenate(
-        [target, stiffness[None], live[None], jnp.zeros((3, cap), jnp.float32)], axis=0
-    )
-    stacked = jnp.concatenate([base_velocity, lax.rsqrt(density)[None]], axis=0)
     groups = [axis_groups(count) for count in mesh_counts]
     number = len(groups[0]) * len(groups[1]) * len(groups[2])
     width = len(groups[1]) * len(groups[2]) * cap
@@ -465,9 +479,16 @@
     return pl.pallas_call(
         functools.partial(kernel, mesh_counts, sizes),
         out_shape=jax.ShapeDtypeStruct((3, cap), jnp.float32),
-        in_specs=[pl.BlockSpec(memory_space=pltpu.VMEM)] * 3,
+        in_specs=[pl.BlockSpec(memory_space=pltpu.HBM)] * 7,
         out_specs=pl.BlockSpec(memory_space=pltpu.VMEM),
         scratch_shapes=[
+            pltpu.VMEM((4, size_x, size_y, size_z), jnp.float32),
+            pltpu.VMEM((size_x, size_y, size_z), jnp.float32),
+            pltpu.VMEM((3, cap), jnp.int32),
+            pltpu.VMEM((3, cap), jnp.float32),
+            pltpu.VMEM((3, cap), jnp.float32),
+            pltpu.VMEM((1, cap), jnp.float32),
+            pltpu.SMEM((1,), jnp.int32),
             pltpu.VMEM((4, size_x + 5, rows_y, lanes), jnp.float32),
             pltpu.VMEM((4, LOW + HIGH, size_y, size_z), jnp.float32),
             pltpu.VMEM((2, 4, size_x + 5, size_y, size_z), jnp.float32),
@@ -476,26 +497,27 @@
             pltpu.VMEM((number, 8, cap), jnp.float32),
             pltpu.VMEM((ITERS, number, 3 * (cap // 128), 128), jnp.float32),
             pltpu.VMEM((ITERS, 3, longest, 2, 128), jnp.float32),
-            pltpu.VMEM((most, 2, 128), jnp.float32),
+            pltpu.VMEM((ITERS, most, 2, 128), jnp.float32),
             pltpu.VMEM((len(groups[0]), tallest * rows_y, width), jnp.float32),
             pltpu.VMEM((len(groups[0]), lanes, width), jnp.bfloat16),
             pltpu.VMEM((len(groups[0]), lanes, width), jnp.bfloat16),
             pltpu.VMEM((3 * tallest * rows_y, width), jnp.bfloat16),
             pltpu.VMEM((3 * tallest * rows_y, width), jnp.bfloat16),
             pltpu.VMEM((3, size_x + 5, rows_y, lanes), jnp.float32),
+            pltpu.SemaphoreType.DMA((7,)),
             pltpu.SemaphoreType.DMA((turns, number - 1)),
             pltpu.SemaphoreType.DMA((turns, number - 1)),
             pltpu.SemaphoreType.DMA((ITERS, 3, longest - 1)),
             pltpu.SemaphoreType.DMA((ITERS, 3, longest - 1)),
-            pltpu.SemaphoreType.DMA((most,)),
-            pltpu.SemaphoreType.DMA((most,)),
+            pltpu.SemaphoreType.DMA((ITERS, most)),
+            pltpu.SemaphoreType.DMA((ITERS, most)),
             pltpu.SemaphoreType.DMA((10,)),
             pltpu.SemaphoreType.DMA((10,)),
         ],
         compiler_params=pltpu.CompilerParams(
             collective_id=0, has_side_effects=True, vmem_limit_bytes=60 * 1024 * 1024
         ),
-    )(stacked, marks, aux)
+    )(density, base_velocity, cells, offsets, target, stiffness[None], counts)
 
 
 def solution(mesh):

time: 73.6 us -> 57 us (0.77)
  Pallas kernels: 66.7 us -> 54.9 us
  other arithmetic: 2.38 us -> 0 us
  local copies, waits for them, and re-layouts: 3.47 us -> 1.28 us
    pallas_call x1, Pallas kernels: 66.7 us -> 54.9 us  [body(): pl.pallas_call(functools.partial(kernel, mesh_counts, sizes), out_shape=j...]
    concatenate x2 -> x0, other arithmetic: 2.23 us -> none  [the longest x1 1.56 us: body(): stacked = jnp.concatenate([base_velocity, lax.rsqrt(density)[None]], axis=0)]
    unnamed x9 -> x1, local copies, waits for them, and re-layouts: 2.55 us -> 1.28 us
    broadcast_in_dim x3 -> x0, local copies, waits for them, and re-layouts: 0.77 us -> none  [the longest x1 0.77 us: body(): stacked = jnp.concatenate([base_velocity, lax.rsqrt(density)[None]], axis=0)]
where the time goes in v1:
time: 57 us; the launch traced here: 56.8 us
  Pallas kernels  54.9 us (96%)
  local copies, waits for them, and re-layouts  1.28 us (2%)
  between operations  0.66 us (1%)
    pallas_call x1, Pallas kernels, body(): pl.pallas_call(functools.partial(kernel, mesh_counts, sizes), out_shape=j...  54.9 us
    unnamed x1, local copies, waits for them, and re-layouts  1.28 us

profile of v1, /device:TPU:0, one launch (start us, length us, event | category | flops | bytes accessed | tf_op | source)
XLA Modules:
  0.0 56.8 jit_solution(12299700462496780556)
XLA Ops:
  0.7 54.9 %shard_map.73 = f32[3,256]{1,0:T(4,128)} custom-call(f32[8,8,128]{2,1,0:T(8,128)} %density_in.1, f32[3,8,8,128]{3,2,1,0:T(8,128)} %velocity_in.1, s32[3,256]{1,0:T(4,128)} %cells_in.1, f32[3,256]{1,0:T(4,128)} %offsets_in.1, f32[3,256]{1,0:T(4,128)} %target_in.1, f32[1,256]{1,0:T(1,128)} %bitcast.1, s32[1]{0:T(128)S(6)} %copy.9.live_in), custom_call_target="tpu_custom_call" | custom-call | tf_op jit(solution)/shard_map/pallas_call | solution.py:479
  55.5 1.3 %copy.10 = f32[3,256]{1,0:T(4,128)} copy(f32[3,256]{1,0:T(4,128)} %shard_map.73) | data formatting | bytes 6144

commit v2 on v1

--- a/solution.py
+++ b/solution.py
@@ -69,16 +69,24 @@
 
 def kernel(
     counts, sizes, density_in, velocity_in, cells_in, offsets_in, target_in, stiffness_in, live_in, out,
-    block, dense, cell, offset, target, stiffness, held, fields, xbuf, ybuf, zpack, zbuf, nbuf, fbuf, rbuf, dbuf, txy, thi, tlo, whi, wlo,
-    grid, lsem, nsend, nrecv, rsend, rrecv, dsend, drecv, hsend, hrecv,
+    block, dense, cell, offset, target, stiffness, held, fields, xbuf, ybuf, zpack, zbuf, nbuf, fbuf, rbuf, dbuf, thi, tlo, tz, tzn, wide,
+    planar, grid, lsem, nsend, nrecv, rsend, rrecv, dsend, drecv, hsend, hrecv,
 ):
     size_x, size_y, size_z = sizes
     cap = cell.shape[1]
     rows_y, lanes = fields.shape[2], fields.shape[3]
     assert 8 * (size_x + 5) <= size_z == lanes - size_z
     wide_x = size_x + 5
+    tall_z, wide_xy = planar.shape[1], planar.shape[2]
     groups = [axis_groups(count) for count in counts]
-    slots = list(itertools.product(*[[offset for offset, _ in group] for group in groups]))
+    near_x, near_y, near_z = (len(group) for group in groups)
+    flat = near_x * near_y
+    places = sorted(
+        itertools.product(range(near_x), range(near_y), range(near_z)),
+        key=lambda place: (place[2] > 0, place[0], place[2], place[1]),
+    )
+    slots = [tuple(group[k][0] for group, k in zip(groups, place)) for place in places]
+    parts = [(1, flat), (flat, len(slots))]
     me = [lax.axis_index(name) for name in AXES]
     sent = []
 
@@ -122,22 +130,24 @@
         return pltpu.make_async_remote_copy(
             src_ref=fbuf.at[turn - 1, 0] if turn else nbuf.at[0],
             dst_ref=fbuf.at[turn - 1, number] if turn else nbuf.at[number],
-            send_sem=nsend.at[turn, number - 1],
-            recv_sem=nrecv.at[turn, number - 1],
+            send_sem=nsend.at[min(turn, 1)],
+            recv_sem=nrecv.at[turn, int(number >= flat)],
             device_id=device(negated(slots[number])),
             device_id_type=MESH_ID,
         )
 
+    def drain(ref, sem):
+        pltpu.make_async_copy(ref, ref, sem).wait()
+
     def send_round(turn):
         for number in sorted(range(1, len(slots)), key=lambda k: (slots[k][0] == 0, k)):
-            copy = neighbour_copy(turn, number)
-            copy.start()
-            sent.append(copy)
-
-    def wait_round(turn, off_x):
-        for number in range(1, len(slots)):
-            if slots[number][0] == off_x:
-                neighbour_copy(turn, number).wait_recv()
+            neighbour_copy(turn, number).start()
+
+    def wait_round(turn, part):
+        first, last = parts[part]
+        if first < last:
+            at = pl.ds(first, last - first)
+            drain(fbuf.at[turn - 1, at] if turn else nbuf.at[at], nrecv.at[turn, part])
 
     def sum_copy(turn, stage, step):
         axis = 2 - stage
@@ -183,8 +193,8 @@
         return pltpu.make_async_remote_copy(
             src_ref=dbuf.at[step, 0],
             dst_ref=dbuf.at[step, number + 1],
-            send_sem=dsend.at[step, number],
-            recv_sem=drecv.at[step, number],
+            send_sem=dsend.at[0],
+            recv_sem=drecv.at[step],
             device_id=device(negated(everyone[number])),
             device_id_type=MESH_ID,
         )
@@ -192,13 +202,10 @@
     def send_directly(step, value):
         dbuf[step, 0] = value
         for number in range(len(everyone)):
-            copy = direct_copy(step, number)
-            copy.start()
-            sent.append(copy)
+            direct_copy(step, number).start()
 
     def wait_directly(step):
-        for number in range(len(everyone)):
-            direct_copy(step, number).wait_recv()
+        drain(dbuf.at[step, pl.ds(1, len(everyone))], drecv.at[step])
         return jnp.sum(dbuf[step], axis=0)
 
     offs_y = sorted({1 % counts[1], (-1) % counts[1]})
@@ -271,84 +278,118 @@
             fields[:, plane, :, pl.ds(0, size_z)] = jnp.where(lane < LOW, first, tall)
             tail = jnp.where(lane < LOW, tall, jnp.where(lane < LOW + HIGH, last, 0.0))
             fields[:, plane, :, pl.ds(size_z, lanes - size_z)] = tail
+        blank = jnp.zeros((wide_xy - wide_x * rows_y, lanes), jnp.float32)
+        for number in range(4):
+            level = jnp.concatenate([fields[number].reshape(wide_x * rows_y, lanes), blank], axis=0)
+            planar[number] = jnp.transpose(level)[:tall_z]
 
     go(along_x + along_y)
     send_round(0)
 
-    def build(xi, yi, zi):
-        number = slots.index((groups[0][xi][0], groups[1][yi][0], groups[2][zi][0]))
+    def reach(xi):
+        start, planes = span(groups[0][xi][1], size_x)
+        first = start * rows_y // 128 * 128
+        return first, round_up((start + planes) * rows_y, 128)
+
+    def build(number):
+        xi, yi, zi = places[number]
         info = nbuf[number]
         cells = [info[k : k + 1] for k in range(3)]
         fours = [weights(info[k + 3 : k + 4]) for k in range(3)]
-        block = (yi * len(groups[2]) + zi) * cap
+        here = number * cap
         start, planes = span(groups[0][xi][1], size_x)
-        first = start // 8 * 8
-        tall = round_up(start + planes - first, 8)
-        tab_x = table(cells[0], fours[0], groups[0][xi][1], size_x, float(first), tall)
+        tab_x = table(cells[0], fours[0], groups[0][xi][1], size_x, 0.0, round_up(wide_x, 8))
         tab_y = table(cells[1], fours[1], groups[1][yi][1], size_y, 0.0, rows_y)
-        for plane in range(planes):
-            at = start - first + plane
-            txy[xi, pl.ds(plane * rows_y, rows_y), pl.ds(block, cap)] = tab_x[at : at + 1] * tab_y
+        low_row, high_row = reach(xi)
+        for plane in range(low_row // rows_y, high_row // rows_y):
+            at = pl.ds(plane * rows_y, rows_y)
+            if start <= plane < start + planes:
+                high, low = split(tab_x[plane : plane + 1] * tab_y)
+            else:
+                high = low = jnp.zeros((rows_y, cap), jnp.bfloat16)
+            thi[at, pl.ds(here, cap)] = high
+            tlo[at, pl.ds(here, cap)] = low
         shifts = groups[2][zi][1]
-        start, planes = span(shifts, size_z)
-        first = start // 16 * 16
-        tall = round_up(start + planes - first, 16)
-        tab_z = table(cells[2], fours[2], shifts, size_z, float(first), tall)
-        high, low = split(tab_z)
-        for ref, part in ((thi, high), (tlo, low)):
-            if first:
-                ref[xi, pl.ds(0, first), pl.ds(block, cap)] = jnp.zeros((first, cap), jnp.bfloat16)
-            ref[xi, pl.ds(first, tall), pl.ds(block, cap)] = part
-            rest = lanes - first - tall
-            if rest:
-                ref[xi, pl.ds(first + tall, rest), pl.ds(block, cap)] = jnp.zeros(
-                    (rest, cap), jnp.bfloat16
-                )
-
-    start_own, planes_own = span(groups[0][0][1], size_x)
+        if zi == 0:
+            tz[:, pl.ds(here, cap)] = table(cells[2], fours[2], shifts, size_z, 0.0, tall_z)
+        else:
+            edge = None
+            for shift in shifts:
+                first = 0.0 if shift < 0 else size_z - 3.0
+                part = table(cells[2], fours[2], [shift], size_z, first, 8)
+                edge = part if edge is None else edge + part
+            tzn[:, pl.ds(here - flat * cap, cap)] = edge
 
     def interpolate(field):
-        rows = planes_own * rows_y
-        high, low = split(field.reshape(3 * rows, lanes))
-        z_high, z_low = thi[0, :, pl.ds(0, cap)], tlo[0, :, pl.ds(0, cap)]
-        part = dot_nn(high, z_high) + dot_nn(low, z_high) + dot_nn(high, z_low)
-        plane = txy[0, pl.ds(0, rows), pl.ds(0, cap)]
+        high, low = split(field.reshape(3 * tall_z, wide_xy))
+        xy_high, xy_low = thi[:, pl.ds(0, cap)], tlo[:, pl.ds(0, cap)]
+        part = dot_nn(high, xy_high) + dot_nn(low, xy_high) + dot_nn(high, xy_low)
+        along = tz[:, pl.ds(0, cap)]
         return jnp.concatenate(
             [
-                jnp.sum(part[c * rows : (c + 1) * rows] * plane, axis=0, keepdims=True)
+                jnp.sum(part[c * tall_z : (c + 1) * tall_z] * along, axis=0, keepdims=True)
                 for c in range(3)
             ],
             axis=0,
         )
 
-    def spread(turn):
-        for xi, (off_x, shifts) in enumerate(groups[0]):
-            start, planes = span(shifts, size_x)
-            rows = planes * rows_y
-            wait_round(turn, off_x)
-            for yi, (off_y, _) in enumerate(groups[1]):
-                for zi, (off_z, _) in enumerate(groups[2]):
-                    number = slots.index((off_x, off_y, off_z))
-                    block = (yi * len(groups[2]) + zi) * cap
-                    plane = txy[xi, pl.ds(0, rows), pl.ds(block, cap)]
-                    for c in range(3):
-                        high, low = split(plane * taken(turn, number, c))
-                        whi[pl.ds(c * rows, rows), pl.ds(block, cap)] = high
-                        wlo[pl.ds(c * rows, rows), pl.ds(block, cap)] = low
-            high, low = whi[pl.ds(0, 3 * rows), :], wlo[pl.ds(0, 3 * rows), :]
-            part = dot_nt(high, thi[xi]) + dot_nt(low, thi[xi]) + dot_nt(high, tlo[xi])
-            part = part.reshape(3, planes, rows_y, lanes)
-            if xi == 0:
-                if start > 0:
-                    grid[:, pl.ds(0, start)] = jnp.zeros((3, start, rows_y, lanes), jnp.float32)
-                rest = wide_x - start - planes
-                if rest > 0:
-                    grid[:, pl.ds(start + planes, rest)] = jnp.zeros(
-                        (3, rest, rows_y, lanes), jnp.float32
-                    )
-                grid[:, pl.ds(start, planes)] = part
-            else:
-                grid[:, pl.ds(start, planes)] += part
+    def fill(number, rows):
+        at = pl.ds(number * cap, cap)
+        along = tz[:, at]
+        for c in range(3):
+            high, low = split(along * rows[c])
+            wide[pl.ds(c * tall_z, tall_z), at] = high
+            wide[pl.ds((3 + c) * tall_z, tall_z), at] = low
+
+    def contract(xi, first, last):
+        low_row, high_row = reach(xi)
+        row, at = pl.ds(low_row, high_row - low_row), pl.ds(first * cap, (last - first) * cap)
+        both_parts = dot_nt(wide[:, at], thi[row, at])
+        half = 3 * tall_z
+        return both_parts[:half] + both_parts[half:] + dot_nt(wide[pl.ds(0, half), at], tlo[row, at])
+
+    def spread(turn, vector):
+        fill(0, [vector[c : c + 1] for c in range(3)])
+        own = contract(0, 0, 1)
+        wait_round(turn, 0)
+        for number in range(1, flat):
+            fill(number, [taken(turn, number, c) for c in range(3)])
+        if near_y > 1:
+            own = own + contract(0, 1, near_y)
+        for c in range(3):
+            grid[c] = own[c * tall_z : (c + 1) * tall_z]
+        for xi in range(1, near_x):
+            low_row, high_row = reach(xi)
+            side = contract(xi, xi * near_y, (xi + 1) * near_y)
+            for c in range(3):
+                grid[c, :, pl.ds(low_row, high_row - low_row)] += side[c * tall_z : (c + 1) * tall_z]
+        if near_z == 1:
+            return
+        wait_round(turn, 1)
+        each = near_y * (near_z - 1)
+        top = (size_z + 1) // 8 * 8
+        for xi in range(near_x):
+            low_row, high_row = reach(xi)
+            row = pl.ds(low_row, high_row - low_row)
+            begin = flat + xi * each
+            rows = [[], [], []]
+            for number in range(begin, begin + each):
+                edge = tzn[:, pl.ds((number - flat) * cap, cap)]
+                for c in range(3):
+                    rows[c].append(edge * taken(turn, number, c))
+            value = jnp.concatenate([jnp.concatenate(line, axis=1) for line in rows], axis=0)
+            rounded = value.astype(jnp.bfloat16).astype(jnp.float32)
+            both_parts = jnp.concatenate([rounded, value - rounded], axis=0).astype(jnp.bfloat16)
+            at = pl.ds(begin * cap, each * cap)
+            part = dot_nt(both_parts, thi[row, at]) + dot_nt(both_parts, tlo[row, at])
+            part = part[:24] + part[24:]
+            line = lax.broadcasted_iota(jnp.int32, (8, high_row - low_row), 0)
+            for c in range(3):
+                edge = part[c * 8 : c * 8 + 8]
+                grid[c, pl.ds(0, 8), row] += jnp.where(line < 4, edge, 0.0)
+                grid[c, pl.ds(top, 8), row] += pltpu.roll(
+                    jnp.where(line < 4, 0.0, edge), (size_z + 1 - top - 4) % 8, 0
+                )
 
     def shifted(value, by, axis):
         return pltpu.roll(value, by % value.shape[axis], axis)
@@ -360,29 +401,30 @@
         up, down = both(value, axis)
         return up + down
 
-    def sub(value, axis):
-        up, down = both(value, axis)
-        return up - down
-
     def respond():
-        scale = fields[3]
+        scale = planar[3]
         mx, my, mz = (scale * grid[c] for c in range(3))
-        slope_y, slope_z = sub(my, 1), sub(mz, 2)
-        sum_x = 2.0 * mx + add(mx, 1) + add(mx, 2)
-        slope = slope_y + slope_z
-        px = sum_x[2:] + sum_x[:-2] + slope[2:] - slope[:-2]
-        slope_x = mx[2:] - mx[:-2]
-        sum_y = (2.0 * my + add(my, 2))[1:-1] + my[2:] + my[:-2]
-        py = add(sum_y, 1) + sub(slope_x + slope_z[1:-1], 1)
-        sum_z = (2.0 * mz + add(mz, 1))[1:-1] + mz[2:] + mz[:-2]
-        pz = add(sum_z, 2) + sub(slope_x + slope_y[1:-1], 2)
-        half = scale[1:-1] * 0.5
-        return jnp.stack(
-            [half * (m[1:-1] + p * (1.0 / 12.0)) for m, p in ((mx, px), (my, py), (mz, pz))]
-        )
+
+        def along(value, step):
+            return pltpu.roll(value, (-step) % wide_xy, 1)
+
+        def paired(total, slope, step):
+            return along(total + slope, step) + along(total - slope, -step)
+
+        my_up, my_down = along(my, 1), along(my, -1)
+        mz_up, mz_down = shifted(mz, -1, 0), shifted(mz, 1, 0)
+        mx_up, mx_down = along(mx, rows_y), along(mx, -rows_y)
+        slope_x, slope_y, slope_z = mx_up - mx_down, my_up - my_down, mz_up - mz_down
+        px = paired(2.0 * mx + along(mx, 1) + along(mx, -1) + add(mx, 0), slope_y + slope_z, rows_y)
+        py = paired(2.0 * my + along(my, rows_y) + along(my, -rows_y) + add(my, 0), slope_x + slope_z, 1)
+        sum_z = 2.0 * mz + along(mz, 1) + along(mz, -1) + along(mz, rows_y) + along(mz, -rows_y)
+        slope = slope_x + slope_y
+        pz = shifted(sum_z + slope, -1, 0) + shifted(sum_z - slope, 1, 0)
+        half = scale * 0.5
+        return jnp.stack([half * (m + p * (1.0 / 12.0)) for m, p in ((mx, px), (my, py), (mz, pz))])
 
     def apply(turn, vector, summing=None):
-        spread(turn)
+        spread(turn, vector)
         if summing is not None:
             send_sum(summing, 1, wait_sum(summing, 0))
         field = respond()
@@ -406,17 +448,16 @@
             jnp.sum(tile[1:2], axis=1, keepdims=True),
         )
 
-    build(0, 0, 0)
+    build(0)
     for copy in along_x:
         copy.wait_recv()
     go(relayed_y)
-    for off_x, _ in groups[0]:
-        wait_round(0, off_x)
-    for xi, yi, zi in itertools.product(*[range(len(group)) for group in groups]):
-        if (xi, yi, zi) != (0, 0, 0):
-            build(xi, yi, zi)
+    for part in range(2):
+        wait_round(0, part)
+    for number in range(1, len(slots)):
+        build(number)
     widen()
-    residual = live * (target[...] - interpolate(fields[pl.ds(0, 3), pl.ds(1, size_x + 3)]))
+    residual = live * (target[...] - interpolate(planar[pl.ds(0, 3)]))
     put(1, residual)
     send_round(1)
 
@@ -461,6 +502,12 @@
     out[...] = answer
     for copy in sent:
         copy.wait_send()
+    if len(slots) > 1:
+        at = pl.ds(1, len(slots) - 1)
+        drain(nbuf.at[at], nsend.at[0])
+        drain(fbuf.at[:, at], nsend.at[1])
+    if direct and everyone:
+        drain(dbuf.at[:, pl.ds(1, len(everyone))], dsend.at[0])
 
 
 def body(mesh_counts, density, base_velocity, cells, offsets, target, stiffness, counts):
@@ -470,8 +517,8 @@
     rows_y, lanes = round_up(size_y + 5, 16), round_up(size_z + 5, 128)
     groups = [axis_groups(count) for count in mesh_counts]
     number = len(groups[0]) * len(groups[1]) * len(groups[2])
-    width = len(groups[1]) * len(groups[2]) * cap
-    tallest = max(span(shifts, size_x)[1] for _, shifts in groups[0])
+    flat = len(groups[0]) * len(groups[1])
+    tall_z, wide_xy = round_up(size_z + 5, 16), round_up((size_x + 5) * rows_y, 128)
     longest = max(mesh_counts)
     turns = ITERS + 1
     devices = mesh_counts[0] * mesh_counts[1] * mesh_counts[2]
@@ -498,19 +545,20 @@
             pltpu.VMEM((ITERS, number, 3 * (cap // 128), 128), jnp.float32),
             pltpu.VMEM((ITERS, 3, longest, 2, 128), jnp.float32),
             pltpu.VMEM((ITERS, most, 2, 128), jnp.float32),
-            pltpu.VMEM((len(groups[0]), tallest * rows_y, width), jnp.float32),
-            pltpu.VMEM((len(groups[0]), lanes, width), jnp.bfloat16),
-            pltpu.VMEM((len(groups[0]), lanes, width), jnp.bfloat16),
-            pltpu.VMEM((3 * tallest * rows_y, width), jnp.bfloat16),
-            pltpu.VMEM((3 * tallest * rows_y, width), jnp.bfloat16),
-            pltpu.VMEM((3, size_x + 5, rows_y, lanes), jnp.float32),
+            pltpu.VMEM((wide_xy, number * cap), jnp.bfloat16),
+            pltpu.VMEM((wide_xy, number * cap), jnp.bfloat16),
+            pltpu.VMEM((tall_z, flat * cap), jnp.float32),
+            pltpu.VMEM((8, max(1, len(groups[2]) - 1) * flat * cap), jnp.float32),
+            pltpu.VMEM((6 * tall_z, flat * cap), jnp.bfloat16),
+            pltpu.VMEM((4, tall_z, wide_xy), jnp.float32),
+            pltpu.VMEM((3, tall_z, wide_xy), jnp.float32),
             pltpu.SemaphoreType.DMA((7,)),
-            pltpu.SemaphoreType.DMA((turns, number - 1)),
-            pltpu.SemaphoreType.DMA((turns, number - 1)),
-            pltpu.SemaphoreType.DMA((ITERS, 3, longest - 1)),
-            pltpu.SemaphoreType.DMA((ITERS, 3, longest - 1)),
-            pltpu.SemaphoreType.DMA((ITERS, most)),
-            pltpu.SemaphoreType.DMA((ITERS, most)),
+            pltpu.SemaphoreType.DMA((2,)),
+            pltpu.SemaphoreType.DMA((turns, 2)),
+            pltpu.SemaphoreType.DMA((ITERS, 3, longest - 1) if most == 1 else (1, 1, 1)),
+            pltpu.SemaphoreType.DMA((ITERS, 3, longest - 1) if most == 1 else (1, 1, 1)),
+            pltpu.SemaphoreType.DMA((1,)),
+            pltpu.SemaphoreType.DMA((ITERS,)),
             pltpu.SemaphoreType.DMA((10,)),
             pltpu.SemaphoreType.DMA((10,)),
         ],

time: 57 us -> 47 us (0.82)
  Pallas kernels: 54.9 us -> 44.9 us
    pallas_call x1, Pallas kernels: 54.9 us -> 44.9 us  [body(): pl.pallas_call(functools.partial(kernel, mesh_counts, sizes), out_shape=j...]
where the time goes in v2:
time: 47 us; the launch traced here: 46.9 us
  Pallas kernels  44.9 us (96%)
  local copies, waits for them, and re-layouts  1.28 us (3%)
  between operations  0.66 us (1%)
    pallas_call x1, Pallas kernels, body(): pl.pallas_call(functools.partial(kernel, mesh_counts, sizes), out_shape=j...  44.9 us
    unnamed x1, local copies, waits for them, and re-layouts  1.28 us

profile of v2, /device:TPU:0, one launch (start us, length us, event | category | flops | bytes accessed | tf_op | source)
XLA Modules:
  0.0 46.9 jit_solution(5533028417645854118)
XLA Ops:
  0.7 44.9 %shard_map.73 = f32[3,256]{1,0:T(4,128)} custom-call(f32[8,8,128]{2,1,0:T(8,128)} %density_in.1, f32[3,8,8,128]{3,2,1,0:T(8,128)} %velocity_in.1, s32[3,256]{1,0:T(4,128)} %cells_in.1, f32[3,256]{1,0:T(4,128)} %offsets_in.1, f32[3,256]{1,0:T(4,128)} %target_in.1, f32[1,256]{1,0:T(1,128)} %bitcast.1, s32[1]{0:T(128)S(6)} %copy.9.live_in), custom_call_target="tpu_custom_call" | custom-call | tf_op jit(solution)/shard_map/pallas_call | solution.py:526
  45.6 1.3 %copy.10 = f32[3,256]{1,0:T(4,128)} copy(f32[3,256]{1,0:T(4,128)} %shard_map.73) | data formatting | bytes 6144

commit v3 on v2

--- a/solution.py
+++ b/solution.py
@@ -11,6 +11,7 @@
 ITERS = 3
 MOST_DIRECT = 64
 LOW, HIGH = 2, 3
+GHOSTS = (((0, 1, 2), 1, 2), ((3,), LOW, HIGH))
 MESH_ID = pl.DeviceIdType.MESH
 AXES = ("gx", "gy", "gz")
 
@@ -46,7 +47,7 @@
     place = lax.broadcasted_iota(jnp.int32, (rows, cell.shape[1]), 0).astype(jnp.float32) + first
     total = None
     for shift in shifts:
-        apart = place - (cell + (1.0 + shift * size))
+        apart = place - (cell + (shift * size - 1.0))
         part = jnp.where(apart == 3.0, four[3], 0.0)
         for number in (2, 1, 0):
             part = jnp.where(apart == float(number), four[number], part)
@@ -69,13 +70,13 @@
 
 def kernel(
     counts, sizes, density_in, velocity_in, cells_in, offsets_in, target_in, stiffness_in, live_in, out,
-    block, dense, cell, offset, target, stiffness, held, fields, xbuf, ybuf, zpack, zbuf, nbuf, fbuf, rbuf, dbuf, thi, tlo, tz, tzn, wide,
-    planar, grid, lsem, nsend, nrecv, rsend, rrecv, dsend, drecv, hsend, hrecv,
+    block, dense, cell, offset, target, stiffness, held, slab, slabs, nbuf, fbuf, rbuf, dbuf, thi, tlo, tz, tzn, wide,
+    planar, grid, lsem, nsend, nrecv, rsend, rrecv, dsend, drecv, ssend, srecv, *ghosts,
 ):
     size_x, size_y, size_z = sizes
     cap = cell.shape[1]
-    rows_y, lanes = fields.shape[2], fields.shape[3]
-    assert 8 * (size_x + 5) <= size_z == lanes - size_z
+    rows_y, low_z = size_y + 8, 8
+    assert size_y == 8
     wide_x = size_x + 5
     tall_z, wide_xy = planar.shape[1], planar.shape[2]
     groups = [axis_groups(count) for count in counts]
@@ -103,6 +104,120 @@
     everyone = [o for o in itertools.product(*[range(n) for n in counts]) if any(o)]
     direct = len(everyone) < MOST_DIRECT
     peers = everyone if direct else sorted(peers)
+    offs_y = sorted({1 % counts[1], (-1) % counts[1]})
+    line = lax.broadcasted_iota(jnp.int32, (8, size_z), 0)
+    wide_line = lax.broadcasted_iota(jnp.int32, (8, wide_xy), 0)
+
+    def halo_copy(sems, number, source, target_ref, offset):
+        return pltpu.make_async_remote_copy(
+            src_ref=source,
+            dst_ref=target_ref,
+            send_sem=sems[0].at[number],
+            recv_sem=sems[1].at[number],
+            device_id=device(negated(offset)),
+            device_id_type=MESH_ID,
+        )
+
+    def exchange(number):
+        (names, low, high), (xl, xh, pack, lpack, hpack, yb, lb, hb, send, recv) = GHOSTS[number], ghosts[10 * number : 10 * number + 10]
+        at, sems = pl.ds(names[0], len(names)), (send, recv)
+        below, above = (-1) % counts[0], 1 % counts[0]
+        copies = []
+        for k, off in enumerate(offs_y):
+            copies += [
+                halo_copy(sems, 2 + 3 * k, pack, yb.at[k], (0, off, 0)),
+                halo_copy(sems, 3 + 3 * k, lpack, lb.at[k], (below, off, 0)),
+                halo_copy(sems, 4 + 3 * k, hpack, hb.at[k], (above, off, 0)),
+            ]
+        copies += [
+            halo_copy(sems, 0, block.at[at, pl.ds(size_x - low, low)], xl, (below, 0, 0)),
+            halo_copy(sems, 1, block.at[at, pl.ds(0, high)], xh, (above, 0, 0)),
+        ]
+        return copies
+
+    def slab_copy(number):
+        return pltpu.make_async_remote_copy(
+            src_ref=slab,
+            dst_ref=slabs.at[number - flat],
+            send_sem=ssend.at[0],
+            recv_sem=srecv.at[0],
+            device_id=device(negated(slots[number])),
+            device_id_type=MESH_ID,
+        )
+
+    def prepare():
+        for number, (names, low, high) in enumerate(GHOSTS):
+            pack, lpack, hpack = ghosts[10 * number + 2 : 10 * number + 5]
+            levels = [size_y - low + j for j in range(low)] + list(range(high))
+            for f, name in enumerate(names):
+                for j, level in enumerate(levels):
+                    kind = f * len(levels) + j
+                    for q in range(size_x):
+                        row = block[name, q, pl.ds(level, 1), :]
+                        pack[kind, pl.ds(q, 1), :] = row
+                        if q >= size_x - low:
+                            lpack[pl.ds(kind * low + q - size_x + low, 1), :] = row
+                        if q < high:
+                            hpack[pl.ds(kind * high + q, 1), :] = row
+        for pair in range(2):
+            level = jnp.concatenate(
+                [block[2 * pair + 1 - half, q] for q in range(size_x) for half in range(2)], axis=0
+            )
+            turned = jnp.transpose(level)
+            slab[pair] = jnp.where(line[:, : rows_y * size_x] < HIGH, turned[:8], turned[size_z - 8 :])
+
+    def assemble(number):
+        (names, low, high), (xl, xh, pack, lpack, hpack, yb, lb, hb, send, recv) = GHOSTS[number], ghosts[10 * number : 10 * number + 10]
+        kinds = low + high
+        k_below, k_above = offs_y.index((-1) % counts[1]), offs_y.index(1 % counts[1])
+        empty = jnp.zeros((8, size_z), jnp.float32)
+
+        def core(f, p):
+            if p < LOW:
+                return xl[f, p - LOW + low] if p >= LOW - low else empty
+            if p < LOW + size_x:
+                return block[names[f], p - LOW]
+            return xh[f, p - LOW - size_x] if p < LOW + size_x + high else empty
+
+        def beside(f, p, j):
+            k, kind = (k_below if j < low else k_above), f * kinds + j
+            if LOW - low <= p < LOW:
+                return lb[k, pl.ds(kind * low + p - LOW + low, 1), :]
+            if LOW <= p < LOW + size_x:
+                return yb[k, kind, pl.ds(p - LOW, 1), :]
+            if LOW + size_x <= p < LOW + size_x + high:
+                return hb[k, pl.ds(kind * high + p - LOW - size_x, 1), :]
+            return None
+
+        lane = lax.broadcasted_iota(jnp.int32, (8, wide_xy), 1) - (8 - LOW)
+        plane, level = lane // rows_y, lane % rows_y
+        blank = jnp.zeros((wide_xy - (wide_x + 1) * rows_y, size_z), jnp.float32)
+        ends = {}
+        for shift_x, shift_y in itertools.product((0, -1, 1), (0, -1, 1)):
+            inside = (lane >= 0) & (plane < wide_x) & (level < size_y + LOW + HIGH)
+            for value, shift, size in ((plane, shift_x, size_x), (level, shift_y, size_y)):
+                inside &= (value >= LOW + shift * size) & (value < LOW + (shift + 1) * size)
+            for shift_z in (-1, 1):
+                offset_of = tuple(o % n for o, n in zip((shift_x, shift_y, shift_z), counts))
+                got = slabs.at[slots.index(offset_of) - flat]
+                for name in names:
+                    by = (shift_x * size_x + LOW) * rows_y + shift_y * size_y + (0, 8)[name % 2]
+                    edge = jnp.concatenate([got[name // 2], jnp.zeros((8, wide_xy - rows_y * size_x), jnp.float32)], axis=1)
+                    edge = pltpu.roll(edge, by % wide_xy, 1)
+                    ends[name, shift_z] = jnp.where(inside, edge, ends.get((name, shift_z), 0.0))
+        for f, name in enumerate(names):
+            tiles = []
+            for p in range(wide_x + 1):
+                ghost = empty
+                for j in range(kinds):
+                    row = beside(f, p, j) if j < low else beside(f, p - 1, j)
+                    if row is not None:
+                        ghost = jnp.where(line == (8 - low + j if j < low else j - low), row, ghost)
+                tiles += [ghost, core(f, p) if p < wide_x else empty]
+            planar[name, pl.ds(low_z, size_z)] = jnp.transpose(jnp.concatenate(tiles + [blank], axis=0))
+            planar[name, pl.ds(0, 8)] = jnp.where(wide_line >= 8 - LOW, ends[name, -1], 0.0)
+            planar[name, pl.ds(low_z + size_z, 8)] = jnp.where(wide_line < HIGH, ends[name, 1], 0.0)
+
     loads = [
         pltpu.make_async_copy(source, target_ref, lsem.at[number])
         for number, (source, target_ref) in enumerate((
@@ -115,9 +230,12 @@
         pl.semaphore_signal(barrier, inc=1, device_id=device(peer), device_id_type=MESH_ID)
     for load in loads:
         load.start()
-    for load in loads:
+    for load in loads[:2]:
         load.wait()
     block[3] = lax.rsqrt(dense[...])
+    prepare()
+    for load in loads[2:]:
+        load.wait()
     corner = [m * size for m, size in zip(me, sizes)]
     for k in range(3):
         nbuf[0, pl.ds(k, 1), :] = (cell[pl.ds(k, 1), :] - corner[k]).astype(jnp.float32)
@@ -208,88 +326,10 @@
         drain(dbuf.at[step, pl.ds(1, len(everyone))], drecv.at[step])
         return jnp.sum(dbuf[step], axis=0)
 
-    offs_y = sorted({1 % counts[1], (-1) % counts[1]})
-    offs_z = sorted({1 % counts[2], (-1) % counts[2]})
-
-    def halo_copy(number, source, target, offset):
-        return pltpu.make_async_remote_copy(
-            src_ref=source,
-            dst_ref=target,
-            send_sem=hsend.at[number],
-            recv_sem=hrecv.at[number],
-            device_id=device(negated(offset)),
-            device_id_type=MESH_ID,
-        )
-
-    def go(copies):
-        for copy in copies:
-            copy.start()
-            sent.append(copy)
-
-    low, high = pl.ds(0, LOW), pl.ds(LOW, HIGH)
-    along_x = [
-        halo_copy(0, block.at[:, pl.ds(size_x - LOW, LOW)], xbuf.at[:, low], (counts[0] - 1, 0, 0)),
-        halo_copy(1, block.at[:, pl.ds(0, HIGH)], xbuf.at[:, high], (1, 0, 0)),
-    ]
-    along_y, relayed_y = [], []
-    for k, off in enumerate(offs_y):
-        here = (0, off, 0)
-        along_y.append(halo_copy(2 + k, block, ybuf.at[k, :, pl.ds(LOW, size_x)], here))
-        relayed_y.append(halo_copy(4 + k, xbuf.at[:, low], ybuf.at[k, :, low], here))
-        relayed_y.append(
-            halo_copy(6 + k, xbuf.at[:, high], ybuf.at[k, :, pl.ds(LOW + size_x, HIGH)], here)
-        )
-    along_z = [halo_copy(8 + k, zpack, zbuf.at[k], (0, 0, off)) for k, off in enumerate(offs_z)]
-
-    def widen():
-        for copy in along_y + relayed_y:
-            copy.wait_recv()
-        below = ybuf.at[offs_y.index((-1) % counts[1])]
-        above = ybuf.at[offs_y.index(1 % counts[1])]
-        lane = lax.broadcasted_iota(jnp.int32, (4, rows_y, size_z), 2)
-        zero = jnp.zeros((4, rows_y - size_y - LOW - HIGH, size_z), jnp.float32)
-        packed = jnp.zeros((4, rows_y, size_z), jnp.float32)
-        for plane in range(wide_x):
-            if plane < LOW:
-                own = xbuf[:, plane]
-            elif plane < LOW + size_x:
-                own = block[:, plane - LOW]
-            else:
-                own = xbuf[:, plane - size_x]
-            tall = jnp.concatenate(
-                [below[:, plane][:, size_y - LOW :], own, above[:, plane][:, :HIGH], zero], axis=1
-            )
-            fields[:, plane, :, pl.ds(0, size_z)] = tall
-            ends = jnp.where(lane < HIGH, tall, pltpu.roll(tall, LOW + HIGH, 2))
-            at = 8 * plane
-            inside = (lane >= at) & (lane < at + LOW + HIGH)
-            packed = jnp.where(inside, pltpu.roll(ends, at, 2) if at else ends, packed)
-        zpack[...] = packed
-        go(along_z)
-        for copy in along_z:
-            copy.wait_recv()
-        before = zbuf[offs_z.index((-1) % counts[2])]
-        after = zbuf[offs_z.index(1 % counts[2])]
-        for plane in range(wide_x):
-            at = 8 * plane
-            tall = pltpu.roll(fields[:, plane, :, pl.ds(0, size_z)], LOW, 2)
-            first = pltpu.roll(before, (-(at + HIGH)) % size_z, 2)
-            last = pltpu.roll(after, (LOW - at) % size_z, 2)
-            fields[:, plane, :, pl.ds(0, size_z)] = jnp.where(lane < LOW, first, tall)
-            tail = jnp.where(lane < LOW, tall, jnp.where(lane < LOW + HIGH, last, 0.0))
-            fields[:, plane, :, pl.ds(size_z, lanes - size_z)] = tail
-        blank = jnp.zeros((wide_xy - wide_x * rows_y, lanes), jnp.float32)
-        for number in range(4):
-            level = jnp.concatenate([fields[number].reshape(wide_x * rows_y, lanes), blank], axis=0)
-            planar[number] = jnp.transpose(level)[:tall_z]
-
-    go(along_x + along_y)
-    send_round(0)
-
     def reach(xi):
         start, planes = span(groups[0][xi][1], size_x)
-        first = start * rows_y // 128 * 128
-        return first, round_up((start + planes) * rows_y, 128)
+        first = (start * rows_y + 8 - LOW) // 128 * 128
+        return first, round_up((start + planes) * rows_y + HIGH, 128)
 
     def build(number):
         xi, yi, zi = places[number]
@@ -298,24 +338,35 @@
         fours = [weights(info[k + 3 : k + 4]) for k in range(3)]
         here = number * cap
         start, planes = span(groups[0][xi][1], size_x)
-        tab_x = table(cells[0], fours[0], groups[0][xi][1], size_x, 0.0, round_up(wide_x, 8))
-        tab_y = table(cells[1], fours[1], groups[1][yi][1], size_y, 0.0, rows_y)
+        tab_x = table(cells[0], fours[0], groups[0][xi][1], size_x, float(-LOW), round_up(wide_x, 8))
+        shifts = groups[1][yi][1]
+        side = lax.broadcasted_iota(jnp.int32, (8, cap), 0)
+        tab_y = table(cells[1], fours[1], shifts, size_y, 0.0, size_y)
+        below = jnp.where(side >= 8 - LOW, table(cells[1], fours[1], shifts, size_y, -8.0, 8), 0.0)
+        above = jnp.where(side < HIGH, table(cells[1], fours[1], shifts, size_y, float(size_y), 8), 0.0)
         low_row, high_row = reach(xi)
         for plane in range(low_row // rows_y, high_row // rows_y):
             at = pl.ds(plane * rows_y, rows_y)
             if start <= plane < start + planes:
-                high, low = split(tab_x[plane : plane + 1] * tab_y)
+                mine = tab_x[plane : plane + 1]
+                ghost = below * mine
+                if plane > start:
+                    ghost = ghost + above * tab_x[plane - 1 : plane]
+                high, low = split(jnp.concatenate([ghost, tab_y * mine], axis=0))
+            elif plane == start + planes:
+                ghost = above * tab_x[plane - 1 : plane]
+                high, low = split(jnp.concatenate([ghost, jnp.zeros_like(ghost)], axis=0))
             else:
                 high = low = jnp.zeros((rows_y, cap), jnp.bfloat16)
             thi[at, pl.ds(here, cap)] = high
             tlo[at, pl.ds(here, cap)] = low
         shifts = groups[2][zi][1]
         if zi == 0:
-            tz[:, pl.ds(here, cap)] = table(cells[2], fours[2], shifts, size_z, 0.0, tall_z)
+            tz[:, pl.ds(here, cap)] = table(cells[2], fours[2], shifts, size_z, float(-low_z), tall_z)
         else:
             edge = None
             for shift in shifts:
-                first = 0.0 if shift < 0 else size_z - 3.0
+                first = float(-LOW) if shift < 0 else size_z - 5.0
                 part = table(cells[2], fours[2], [shift], size_z, first, 8)
                 edge = part if edge is None else edge + part
             tzn[:, pl.ds(here - flat * cap, cap)] = edge
@@ -367,7 +418,6 @@
             return
         wait_round(turn, 1)
         each = near_y * (near_z - 1)
-        top = (size_z + 1) // 8 * 8
         for xi in range(near_x):
             low_row, high_row = reach(xi)
             row = pl.ds(low_row, high_row - low_row)
@@ -383,13 +433,14 @@
             at = pl.ds(begin * cap, each * cap)
             part = dot_nt(both_parts, thi[row, at]) + dot_nt(both_parts, tlo[row, at])
             part = part[:24] + part[24:]
-            line = lax.broadcasted_iota(jnp.int32, (8, high_row - low_row), 0)
+            which = wide_line[:, : high_row - low_row]
             for c in range(3):
                 edge = part[c * 8 : c * 8 + 8]
-                grid[c, pl.ds(0, 8), row] += jnp.where(line < 4, edge, 0.0)
-                grid[c, pl.ds(top, 8), row] += pltpu.roll(
-                    jnp.where(line < 4, 0.0, edge), (size_z + 1 - top - 4) % 8, 0
-                )
+                early, late = pltpu.roll(edge, 6, 0), pltpu.roll(edge, 3, 0)
+                grid[c, pl.ds(0, 8), row] += jnp.where(which >= 6, early, 0.0)
+                grid[c, pl.ds(low_z, 8), row] += jnp.where(which < 2, early, 0.0)
+                grid[c, pl.ds(size_z, 8), row] += jnp.where(which == 7, late, 0.0)
+                grid[c, pl.ds(low_z + size_z, 8), row] += jnp.where(which < 3, late, 0.0)
 
     def shifted(value, by, axis):
         return pltpu.roll(value, by % value.shape[axis], axis)
@@ -448,18 +499,29 @@
             jnp.sum(tile[1:2], axis=1, keepdims=True),
         )
 
+    halos = [exchange(number) for number in range(2)]
+    for copy in halos[0]:
+        copy.start()
+    for number in range(flat, len(slots)):
+        slab_copy(number).start()
+    send_round(0)
+    for copy in halos[1]:
+        copy.start()
     build(0)
-    for copy in along_x:
+    drain(slabs, srecv.at[0])
+    for copy in halos[0]:
         copy.wait_recv()
-    go(relayed_y)
+    assemble(0)
+    residual = live * (target[...] - interpolate(planar[pl.ds(0, 3)]))
+    put(1, residual)
+    send_round(1)
     for part in range(2):
         wait_round(0, part)
     for number in range(1, len(slots)):
         build(number)
-    widen()
-    residual = live * (target[...] - interpolate(planar[pl.ds(0, 3)]))
-    put(1, residual)
-    send_round(1)
+    for copy in halos[1]:
+        copy.wait_recv()
+    assemble(1)
 
     image = apply(1, residual)
     direction, along, along_image = residual, image, None
@@ -500,8 +562,9 @@
             residual = residual - alpha * along
             image = image - alpha * along_image
     out[...] = answer
-    for copy in sent:
+    for copy in halos[0] + halos[1] + sent:
         copy.wait_send()
+    drain(slabs, ssend.at[0])
     if len(slots) > 1:
         at = pl.ds(1, len(slots) - 1)
         drain(nbuf.at[at], nsend.at[0])
@@ -510,15 +573,26 @@
         drain(dbuf.at[:, pl.ds(1, len(everyone))], dsend.at[0])
 
 
+def ghost_scratch(sizes, names, low, high):
+    size_x, size_y, size_z = sizes
+    fields, kinds = len(names), len(names) * (low + high)
+    shapes = [
+        (fields, low, size_y, size_z), (fields, high, size_y, size_z),
+        (kinds, size_x, size_z), (kinds * low, size_z), (kinds * high, size_z),
+        (2, kinds, size_x, size_z), (2, kinds * low, size_z), (2, kinds * high, size_z),
+    ]
+    return [pltpu.VMEM(shape, jnp.float32) for shape in shapes] + [pltpu.SemaphoreType.DMA((8,))] * 2
+
+
 def body(mesh_counts, density, base_velocity, cells, offsets, target, stiffness, counts):
     sizes = density.shape
     size_x, size_y, size_z = sizes
     cap = cells.shape[1]
-    rows_y, lanes = round_up(size_y + 5, 16), round_up(size_z + 5, 128)
+    rows_y = size_y + 8
     groups = [axis_groups(count) for count in mesh_counts]
     number = len(groups[0]) * len(groups[1]) * len(groups[2])
     flat = len(groups[0]) * len(groups[1])
-    tall_z, wide_xy = round_up(size_z + 5, 16), round_up((size_x + 5) * rows_y, 128)
+    tall_z, wide_xy = size_z + 16, round_up((size_x + 6) * rows_y, 128)
     longest = max(mesh_counts)
     turns = ITERS + 1
     devices = mesh_counts[0] * mesh_counts[1] * mesh_counts[2]
@@ -536,11 +610,8 @@
             pltpu.VMEM((3, cap), jnp.float32),
             pltpu.VMEM((1, cap), jnp.float32),
             pltpu.SMEM((1,), jnp.int32),
-            pltpu.VMEM((4, size_x + 5, rows_y, lanes), jnp.float32),
-            pltpu.VMEM((4, LOW + HIGH, size_y, size_z), jnp.float32),
-            pltpu.VMEM((2, 4, size_x + 5, size_y, size_z), jnp.float32),
-            pltpu.VMEM((4, rows_y, size_z), jnp.float32),
-            pltpu.VMEM((2, 4, rows_y, size_z), jnp.float32),
+            pltpu.VMEM((2, 8, rows_y * size_x), jnp.float32),
+            pltpu.VMEM((number - flat, 2, 8, rows_y * size_x), jnp.float32),
             pltpu.VMEM((number, 8, cap), jnp.float32),
             pltpu.VMEM((ITERS, number, 3 * (cap // 128), 128), jnp.float32),
             pltpu.VMEM((ITERS, 3, longest, 2, 128), jnp.float32),
@@ -559,9 +630,9 @@
             pltpu.SemaphoreType.DMA((ITERS, 3, longest - 1) if most == 1 else (1, 1, 1)),
             pltpu.SemaphoreType.DMA((1,)),
             pltpu.SemaphoreType.DMA((ITERS,)),
-            pltpu.SemaphoreType.DMA((10,)),
-            pltpu.SemaphoreType.DMA((10,)),
-        ],
+            pltpu.SemaphoreType.DMA((1,)),
+            pltpu.SemaphoreType.DMA((1,)),
+        ] + [item for group in GHOSTS for item in ghost_scratch(sizes, *group)],
         compiler_params=pltpu.CompilerParams(
             collective_id=0, has_side_effects=True, vmem_limit_bytes=60 * 1024 * 1024
         ),

time: 47 us -> 41.1 us (0.87)
  Pallas kernels: 44.9 us -> 39 us
    pallas_call x1, Pallas kernels: 44.9 us -> 39 us  [body(): pl.pallas_call(functools.partial(kernel, mesh_counts, sizes), out_shape=j...]
where the time goes in v3:
time: 41.1 us; the launch traced here: 40.9 us
  Pallas kernels  39 us (95%)
  local copies, waits for them, and re-layouts  1.28 us (3%)
  between operations  0.66 us (2%)
    pallas_call x1, Pallas kernels, body(): pl.pallas_call(functools.partial(kernel, mesh_counts, sizes), out_shape=j...  39 us
    unnamed x1, local copies, waits for them, and re-layouts  1.28 us

profile of v3, /device:TPU:0, one launch (start us, length us, event | category | flops | bytes accessed | tf_op | source)
XLA Modules:
  0.0 40.9 jit_solution(11349388431163783589)
XLA Ops:
  0.7 39.0 %shard_map.73 = f32[3,256]{1,0:T(4,128)} custom-call(f32[8,8,128]{2,1,0:T(8,128)} %density_in.1, f32[3,8,8,128]{3,2,1,0:T(8,128)} %velocity_in.1, s32[3,256]{1,0:T(4,128)} %cells_in.1, f32[3,256]{1,0:T(4,128)} %offsets_in.1, f32[3,256]{1,0:T(4,128)} %target_in.1, f32[1,256]{1,0:T(1,128)} %bitcast.1, s32[1]{0:T(128)S(6)} %copy.9.live_in), custom_call_target="tpu_custom_call" | custom-call | tf_op jit(solution)/shard_map/pallas_call | solution.py:600
  39.7 1.3 %copy.10 = f32[3,256]{1,0:T(4,128)} copy(f32[3,256]{1,0:T(4,128)} %shard_map.73) | data formatting | bytes 6144

commit v4 on v3

--- a/solution.py
+++ b/solution.py
@@ -10,6 +10,7 @@
 
 ITERS = 3
 MOST_DIRECT = 64
+RESPOND_TILES = 6
 LOW, HIGH = 2, 3
 GHOSTS = (((0, 1, 2), 1, 2), ((3,), LOW, HIGH))
 MESH_ID = pl.DeviceIdType.MESH
@@ -84,10 +85,15 @@
     flat = near_x * near_y
     places = sorted(
         itertools.product(range(near_x), range(near_y), range(near_z)),
-        key=lambda place: (place[2] > 0, place[0], place[2], place[1]),
+        key=lambda place: (place[0] > 0, place[2] > 0, place[0], place[2], place[1]),
     )
     slots = [tuple(group[k][0] for group, k in zip(groups, place)) for place in places]
-    parts = [(1, flat), (flat, len(slots))]
+    each = near_y * (near_z - 1)
+    middle = near_y * near_z
+    parts = [(1, middle), (middle, middle + flat - near_y), (middle + flat - near_y, len(slots))]
+    part_of = {number: k for k, part in enumerate(parts) for number in range(*part)}
+    edges = [number for number, place in enumerate(places) if place[2]]
+    farthest = sorted(range(1, len(slots)), key=lambda k: (-sum(map(bool, slots[k])), slots[k][0] == 0, k))
     me = [lax.axis_index(name) for name in AXES]
     sent = []
 
@@ -101,7 +107,10 @@
     for axis, count in enumerate(counts):
         for step in range(1, count):
             peers.add(tuple(step if a == axis else 0 for a in range(3)))
-    everyone = [o for o in itertools.product(*[range(n) for n in counts]) if any(o)]
+    everyone = sorted(
+        (o for o in itertools.product(*[range(n) for n in counts]) if any(o)),
+        key=lambda offset: -sum(min(o, n - o) for o, n in zip(offset, counts)),
+    )
     direct = len(everyone) < MOST_DIRECT
     peers = everyone if direct else sorted(peers)
     offs_y = sorted({1 % counts[1], (-1) % counts[1]})
@@ -138,7 +147,7 @@
     def slab_copy(number):
         return pltpu.make_async_remote_copy(
             src_ref=slab,
-            dst_ref=slabs.at[number - flat],
+            dst_ref=slabs.at[edges.index(number)],
             send_sem=ssend.at[0],
             recv_sem=srecv.at[0],
             device_id=device(negated(slots[number])),
@@ -199,7 +208,7 @@
                 inside &= (value >= LOW + shift * size) & (value < LOW + (shift + 1) * size)
             for shift_z in (-1, 1):
                 offset_of = tuple(o % n for o, n in zip((shift_x, shift_y, shift_z), counts))
-                got = slabs.at[slots.index(offset_of) - flat]
+                got = slabs.at[edges.index(slots.index(offset_of))]
                 for name in names:
                     by = (shift_x * size_x + LOW) * rows_y + shift_y * size_y + (0, 8)[name % 2]
                     edge = jnp.concatenate([got[name // 2], jnp.zeros((8, wide_xy - rows_y * size_x), jnp.float32)], axis=1)
@@ -249,7 +258,7 @@
             src_ref=fbuf.at[turn - 1, 0] if turn else nbuf.at[0],
             dst_ref=fbuf.at[turn - 1, number] if turn else nbuf.at[number],
             send_sem=nsend.at[min(turn, 1)],
-            recv_sem=nrecv.at[turn, int(number >= flat)],
+            recv_sem=nrecv.at[turn, part_of[number]],
             device_id=device(negated(slots[number])),
             device_id_type=MESH_ID,
         )
@@ -258,7 +267,7 @@
         pltpu.make_async_copy(ref, ref, sem).wait()
 
     def send_round(turn):
-        for number in sorted(range(1, len(slots)), key=lambda k: (slots[k][0] == 0, k)):
+        for number in farthest:
             neighbour_copy(turn, number).start()
 
     def wait_round(turn, part):
@@ -362,69 +371,79 @@
             tlo[at, pl.ds(here, cap)] = low
         shifts = groups[2][zi][1]
         if zi == 0:
-            tz[:, pl.ds(here, cap)] = table(cells[2], fours[2], shifts, size_z, float(-low_z), tall_z)
+            tz[:, pl.ds((xi * near_y + yi) * cap, cap)] = table(cells[2], fours[2], shifts, size_z, float(-low_z), tall_z)
         else:
             edge = None
             for shift in shifts:
                 first = float(-LOW) if shift < 0 else size_z - 5.0
                 part = table(cells[2], fours[2], [shift], size_z, first, 8)
                 edge = part if edge is None else edge + part
-            tzn[:, pl.ds(here - flat * cap, cap)] = edge
+            tzn[:, pl.ds(edges.index(number) * cap, cap)] = edge
 
     def interpolate(field):
-        high, low = split(field.reshape(3 * tall_z, wide_xy))
+        high, low = split(field)
         xy_high, xy_low = thi[:, pl.ds(0, cap)], tlo[:, pl.ds(0, cap)]
-        part = dot_nn(high, xy_high) + dot_nn(low, xy_high) + dot_nn(high, xy_low)
-        along = tz[:, pl.ds(0, cap)]
+        both_parts = dot_nn(jnp.concatenate([high, low], axis=0), xy_high)
+        part = both_parts[: 3 * tall_z] + both_parts[3 * tall_z :] + dot_nn(high, xy_low)
+        heights = tz[:, pl.ds(0, cap)]
         return jnp.concatenate(
             [
-                jnp.sum(part[c * tall_z : (c + 1) * tall_z] * along, axis=0, keepdims=True)
+                jnp.sum(part[c * tall_z : (c + 1) * tall_z] * heights, axis=0, keepdims=True)
                 for c in range(3)
             ],
             axis=0,
         )
 
     def fill(number, rows):
-        at = pl.ds(number * cap, cap)
-        along = tz[:, at]
+        xi, yi, _ = places[number]
+        at = pl.ds((xi * near_y + yi) * cap, cap)
+        heights = tz[:, at]
         for c in range(3):
-            high, low = split(along * rows[c])
+            high, low = split(heights * rows[c])
             wide[pl.ds(c * tall_z, tall_z), at] = high
             wide[pl.ds((3 + c) * tall_z, tall_z), at] = low
 
-    def contract(xi, first, last):
+    def contract(first, last):
+        xi, yi, _ = places[first]
         low_row, high_row = reach(xi)
-        row, at = pl.ds(low_row, high_row - low_row), pl.ds(first * cap, (last - first) * cap)
-        both_parts = dot_nt(wide[:, at], thi[row, at])
+        row, count = pl.ds(low_row, high_row - low_row), (last - first) * cap
+        at, here = pl.ds(first * cap, count), pl.ds((xi * near_y + yi) * cap, count)
+        both_parts = dot_nt(wide[:, here], thi[row, at])
         half = 3 * tall_z
-        return both_parts[:half] + both_parts[half:] + dot_nt(wide[pl.ds(0, half), at], tlo[row, at])
+        return both_parts[:half] + both_parts[half:] + dot_nt(wide[pl.ds(0, half), here], tlo[row, at])
 
     def spread(turn, vector):
         fill(0, [vector[c : c + 1] for c in range(3)])
-        own = contract(0, 0, 1)
+        own = contract(0, 1)
         wait_round(turn, 0)
-        for number in range(1, flat):
+        for number in range(1, near_y):
             fill(number, [taken(turn, number, c) for c in range(3)])
         if near_y > 1:
-            own = own + contract(0, 1, near_y)
+            own = own + contract(1, near_y)
         for c in range(3):
             grid[c] = own[c * tall_z : (c + 1) * tall_z]
+        spread_edges(turn, 0)
+        wait_round(turn, 1)
         for xi in range(1, near_x):
+            first = middle + (xi - 1) * near_y
+            for number in range(first, first + near_y):
+                fill(number, [taken(turn, number, c) for c in range(3)])
             low_row, high_row = reach(xi)
-            side = contract(xi, xi * near_y, (xi + 1) * near_y)
+            side = contract(first, first + near_y)
             for c in range(3):
                 grid[c, :, pl.ds(low_row, high_row - low_row)] += side[c * tall_z : (c + 1) * tall_z]
-        if near_z == 1:
-            return
-        wait_round(turn, 1)
-        each = near_y * (near_z - 1)
-        for xi in range(near_x):
+        wait_round(turn, 2)
+        for xi in range(1, near_x):
+            spread_edges(turn, xi)
+
+    def spread_edges(turn, xi):
+        if each:
             low_row, high_row = reach(xi)
             row = pl.ds(low_row, high_row - low_row)
-            begin = flat + xi * each
+            begin = edges[xi * each]
             rows = [[], [], []]
             for number in range(begin, begin + each):
-                edge = tzn[:, pl.ds((number - flat) * cap, cap)]
+                edge = tzn[:, pl.ds(edges.index(number) * cap, cap)]
                 for c in range(3):
                     rows[c].append(edge * taken(turn, number, c))
             value = jnp.concatenate([jnp.concatenate(line, axis=1) for line in rows], axis=0)
@@ -442,37 +461,37 @@
                 grid[c, pl.ds(size_z, 8), row] += jnp.where(which == 7, late, 0.0)
                 grid[c, pl.ds(low_z + size_z, 8), row] += jnp.where(which < 3, late, 0.0)
 
-    def shifted(value, by, axis):
-        return pltpu.roll(value, by % value.shape[axis], axis)
-
-    def both(value, axis):
-        return shifted(value, -1, axis), shifted(value, 1, axis)
-
-    def add(value, axis):
-        up, down = both(value, axis)
-        return up + down
+    def slide(value, step):
+        return pltpu.roll(value, (-step) % wide_xy, 1)
 
     def respond():
-        scale = planar[3]
-        mx, my, mz = (scale * grid[c] for c in range(3))
-
-        def along(value, step):
-            return pltpu.roll(value, (-step) % wide_xy, 1)
-
-        def paired(total, slope, step):
-            return along(total + slope, step) + along(total - slope, -step)
-
-        my_up, my_down = along(my, 1), along(my, -1)
-        mz_up, mz_down = shifted(mz, -1, 0), shifted(mz, 1, 0)
-        mx_up, mx_down = along(mx, rows_y), along(mx, -rows_y)
-        slope_x, slope_y, slope_z = mx_up - mx_down, my_up - my_down, mz_up - mz_down
-        px = paired(2.0 * mx + along(mx, 1) + along(mx, -1) + add(mx, 0), slope_y + slope_z, rows_y)
-        py = paired(2.0 * my + along(my, rows_y) + along(my, -rows_y) + add(my, 0), slope_x + slope_z, 1)
-        sum_z = 2.0 * mz + along(mz, 1) + along(mz, -1) + along(mz, rows_y) + along(mz, -rows_y)
-        slope = slope_x + slope_y
-        pz = shifted(sum_z + slope, -1, 0) + shifted(sum_z - slope, 1, 0)
-        half = scale * 0.5
-        return jnp.stack([half * (m + p * (1.0 / 12.0)) for m, p in ((mx, px), (my, py), (mz, pz))])
+        count = tall_z // 8
+        scales = [planar[3, pl.ds(8 * k, 8)] for k in range(count)]
+        moved = [[scales[k] * grid[c, pl.ds(8 * k, 8)] for k in range(count)] for c in range(3)]
+        result = [[], [], []]
+
+        def shifted(c, k, step):
+            near = moved[c][min(max(k + step, 0), count - 1)]
+            return pltpu.roll(jnp.where(wide_line == (0 if step > 0 else 7), near, moved[c][k]), (-step) % 8, 0)
+
+        for first_tile in range(0, count, RESPOND_TILES):
+            span_of = range(first_tile, min(first_tile + RESPOND_TILES, count))
+            here = [jnp.concatenate([moved[c][k] for k in span_of], axis=0) for c in range(3)]
+            up = [jnp.concatenate([shifted(c, k, 1) for k in span_of], axis=0) for c in range(3)]
+            down = [jnp.concatenate([shifted(c, k, -1) for k in span_of], axis=0) for c in range(3)]
+            (mx, my, mz), (sx, sy, sz) = here, [u + d for u, d in zip(up, down)]
+            dx, dy, dz = [u - d for u, d in zip(up, down)]
+            first, second = slide(mx + my, 1) + slide(mx - my, -1), slide(mx - my, 1) + slide(mx + my, -1)
+            twice = 2.0 * mx + sx
+            px = slide(twice + first + dz, rows_y) + slide(twice + second - dz, -rows_y)
+            first, second = slide(my + mx, rows_y) + slide(my - mx, -rows_y), slide(my - mx, rows_y) + slide(my + mx, -rows_y)
+            twice = 2.0 * my + sy
+            py = slide(twice + first + dz, 1) + slide(twice + second - dz, -1)
+            pz = 2.0 * sz + slide(sz + dx, rows_y) + slide(sz - dx, -rows_y) + slide(sz + dy, 1) + slide(sz - dy, -1)
+            half = 0.5 * jnp.concatenate([scales[k] for k in span_of], axis=0)
+            for c, (m, p) in enumerate(((mx, px), (my, py), (mz, pz))):
+                result[c].append(half * (m + p * (1.0 / 12.0)))
+        return jnp.concatenate(result[0] + result[1] + result[2], axis=0)
 
     def apply(turn, vector, summing=None):
         spread(turn, vector)
@@ -502,7 +521,7 @@
     halos = [exchange(number) for number in range(2)]
     for copy in halos[0]:
         copy.start()
-    for number in range(flat, len(slots)):
+    for number in (k for k in farthest if k in edges):
         slab_copy(number).start()
     send_round(0)
     for copy in halos[1]:
@@ -512,10 +531,10 @@
     for copy in halos[0]:
         copy.wait_recv()
     assemble(0)
-    residual = live * (target[...] - interpolate(planar[pl.ds(0, 3)]))
+    residual = live * (target[...] - interpolate(planar[pl.ds(0, 3)].reshape(3 * tall_z, wide_xy)))
     put(1, residual)
     send_round(1)
-    for part in range(2):
+    for part in range(3):
         wait_round(0, part)
     for number in range(1, len(slots)):
         build(number)
@@ -599,7 +618,7 @@
     most = devices if devices <= MOST_DIRECT else 1
     return pl.pallas_call(
         functools.partial(kernel, mesh_counts, sizes),
-        out_shape=jax.ShapeDtypeStruct((3, cap), jnp.float32),
+        out_shape=pltpu.VMEM((3, cap), jnp.float32),
         in_specs=[pl.BlockSpec(memory_space=pltpu.HBM)] * 7,
         out_specs=pl.BlockSpec(memory_space=pltpu.VMEM),
         scratch_shapes=[
@@ -625,7 +644,7 @@
             pltpu.VMEM((3, tall_z, wide_xy), jnp.float32),
             pltpu.SemaphoreType.DMA((7,)),
             pltpu.SemaphoreType.DMA((2,)),
-            pltpu.SemaphoreType.DMA((turns, 2)),
+            pltpu.SemaphoreType.DMA((turns, 3)),
             pltpu.SemaphoreType.DMA((ITERS, 3, longest - 1) if most == 1 else (1, 1, 1)),
             pltpu.SemaphoreType.DMA((ITERS, 3, longest - 1) if most == 1 else (1, 1, 1)),
             pltpu.SemaphoreType.DMA((1,)),

time: 41.1 us -> 37.9 us (0.922)
  Pallas kernels: 39 us -> 36.5 us
  local copies, waits for them, and re-layouts: 1.28 us -> 0.6 us
    pallas_call x1, Pallas kernels: 39 us -> 36.5 us  [body(): pl.pallas_call(functools.partial(kernel, mesh_counts, sizes), out_shape=p...]
    unnamed x1, local copies, waits for them, and re-layouts: 1.28 us -> 0.6 us
where the time goes in v4:
time: 37.9 us; the launch traced here: 37.8 us
  Pallas kernels  36.5 us (96%)
  between operations  0.66 us (2%)
  local copies, waits for them, and re-layouts  0.6 us (2%)
    pallas_call x1, Pallas kernels, body(): pl.pallas_call(functools.partial(kernel, mesh_counts, sizes), out_shape=p...  36.5 us

profile of v4, /device:TPU:0, one launch (start us, length us, event | category | flops | bytes accessed | tf_op | source)
XLA Modules:
  0.0 37.8 jit_solution(5992079760569351868)
XLA Ops:
  0.7 36.5 %shard_map.73 = f32[3,256]{1,0:T(4,128)S(1)} custom-call(f32[8,8,128]{2,1,0:T(8,128)} %density_in.1, f32[3,8,8,128]{3,2,1,0:T(8,128)} %velocity_in.1, s32[3,256]{1,0:T(4,128)} %cells_in.1, f32[3,256]{1,0:T(4,128)} %offsets_in.1, f32[3,256]{1,0:T(4,128)} %target_in.1, f32[1,256]{1,0:T(1,128)} %bitcast.1, s32[1]{0:T(128)S(6)} %copy.10.live_in), custom_call_target="tpu_custom_call" | custom-call | tf_op jit(solution)/shard_map/pallas_call | solution.py:619
  37.2 0.6 %copy.9 = f32[3,256]{1,0:T(4,128)} copy(f32[3,256]{1,0:T(4,128)S(1)} %shard_map.73) | data formatting | bytes 6144

commit v5 on v4

--- a/solution.py
+++ b/solution.py
@@ -10,7 +10,8 @@
 
 ITERS = 3
 MOST_DIRECT = 64
-RESPOND_TILES = 6
+RESPOND_TILES = 9
+STAGES = 3
 LOW, HIGH = 2, 3
 GHOSTS = (((0, 1, 2), 1, 2), ((3,), LOW, HIGH))
 MESH_ID = pl.DeviceIdType.MESH
@@ -83,14 +84,23 @@
     groups = [axis_groups(count) for count in counts]
     near_x, near_y, near_z = (len(group) for group in groups)
     flat = near_x * near_y
+
+    def stage(place):
+        x, y, z = place
+        if z:
+            return 2 if x else 0
+        return 1 if x else 0
+
     places = sorted(
         itertools.product(range(near_x), range(near_y), range(near_z)),
-        key=lambda place: (place[0] > 0, place[2] > 0, place[0], place[2], place[1]),
+        key=lambda place: (stage(place), place[2] > 0, place[0], place[2], place[1]),
     )
     slots = [tuple(group[k][0] for group, k in zip(groups, place)) for place in places]
     each = near_y * (near_z - 1)
-    middle = near_y * near_z
-    parts = [(1, middle), (middle, middle + flat - near_y), (middle + flat - near_y, len(slots))]
+    parts = []
+    for number in range(STAGES):
+        inside = [k for k, place in enumerate(places) if k and stage(place) == number]
+        parts.append((inside[0], inside[-1] + 1) if inside else (0, 0))
     part_of = {number: k for k, part in enumerate(parts) for number in range(*part)}
     edges = [number for number, place in enumerate(places) if place[2]]
     farthest = sorted(range(1, len(slots)), key=lambda k: (-sum(map(bool, slots[k])), slots[k][0] == 0, k))
@@ -117,30 +127,30 @@
     line = lax.broadcasted_iota(jnp.int32, (8, size_z), 0)
     wide_line = lax.broadcasted_iota(jnp.int32, (8, wide_xy), 0)
 
-    def halo_copy(sems, number, source, target_ref, offset):
+    def halo_copy(sems, source, target_ref, offset):
         return pltpu.make_async_remote_copy(
             src_ref=source,
             dst_ref=target_ref,
-            send_sem=sems[0].at[number],
-            recv_sem=sems[1].at[number],
+            send_sem=sems[0].at[0],
+            recv_sem=sems[1].at[0],
             device_id=device(negated(offset)),
             device_id_type=MESH_ID,
         )
 
     def exchange(number):
-        (names, low, high), (xl, xh, pack, lpack, hpack, yb, lb, hb, send, recv) = GHOSTS[number], ghosts[10 * number : 10 * number + 10]
+        (names, low, high), (xl, xh, pack, lpack, hpack, yb, lb, hb, tally, send, recv) = GHOSTS[number], ghosts[11 * number : 11 * number + 11]
         at, sems = pl.ds(names[0], len(names)), (send, recv)
         below, above = (-1) % counts[0], 1 % counts[0]
         copies = []
         for k, off in enumerate(offs_y):
             copies += [
-                halo_copy(sems, 2 + 3 * k, pack, yb.at[k], (0, off, 0)),
-                halo_copy(sems, 3 + 3 * k, lpack, lb.at[k], (below, off, 0)),
-                halo_copy(sems, 4 + 3 * k, hpack, hb.at[k], (above, off, 0)),
+                halo_copy(sems, pack, yb.at[k], (0, off, 0)),
+                halo_copy(sems, lpack, lb.at[k], (below, off, 0)),
+                halo_copy(sems, hpack, hb.at[k], (above, off, 0)),
             ]
         copies += [
-            halo_copy(sems, 0, block.at[at, pl.ds(size_x - low, low)], xl, (below, 0, 0)),
-            halo_copy(sems, 1, block.at[at, pl.ds(0, high)], xh, (above, 0, 0)),
+            halo_copy(sems, block.at[at, pl.ds(size_x - low, low)], xl, (below, 0, 0)),
+            halo_copy(sems, block.at[at, pl.ds(0, high)], xh, (above, 0, 0)),
         ]
         return copies
 
@@ -156,7 +166,7 @@
 
     def prepare():
         for number, (names, low, high) in enumerate(GHOSTS):
-            pack, lpack, hpack = ghosts[10 * number + 2 : 10 * number + 5]
+            pack, lpack, hpack = ghosts[11 * number + 2 : 11 * number + 5]
             levels = [size_y - low + j for j in range(low)] + list(range(high))
             for f, name in enumerate(names):
                 for j, level in enumerate(levels):
@@ -176,7 +186,7 @@
             slab[pair] = jnp.where(line[:, : rows_y * size_x] < HIGH, turned[:8], turned[size_z - 8 :])
 
     def assemble(number):
-        (names, low, high), (xl, xh, pack, lpack, hpack, yb, lb, hb, send, recv) = GHOSTS[number], ghosts[10 * number : 10 * number + 10]
+        (names, low, high), (xl, xh, pack, lpack, hpack, yb, lb, hb, tally, send, recv) = GHOSTS[number], ghosts[11 * number : 11 * number + 11]
         kinds = low + high
         k_below, k_above = offs_y.index((-1) % counts[1]), offs_y.index(1 % counts[1])
         empty = jnp.zeros((8, size_z), jnp.float32)
@@ -235,10 +245,10 @@
         ))
     ]
     barrier = pltpu.get_barrier_semaphore()
+    for load in loads:
+        load.start()
     for peer in peers:
         pl.semaphore_signal(barrier, inc=1, device_id=device(peer), device_id_type=MESH_ID)
-    for load in loads:
-        load.start()
     for load in loads[:2]:
         load.wait()
     block[3] = lax.rsqrt(dense[...])
@@ -380,11 +390,20 @@
                 edge = part if edge is None else edge + part
             tzn[:, pl.ds(edges.index(number) * cap, cap)] = edge
 
+    def halved(rows, table_high, table_low, dot):
+        count = 3 * tall_z
+        middle = round_up(count // 2, 16)
+        pieces = []
+        for a, b in ((0, middle), (middle, count)):
+            high, low = rows(a, b)
+            both_parts = dot(jnp.concatenate([high, low], axis=0), table_high)
+            pieces.append(both_parts[: b - a] + both_parts[b - a :] + dot(high, table_low))
+        return jnp.concatenate(pieces, axis=0)
+
     def interpolate(field):
         high, low = split(field)
         xy_high, xy_low = thi[:, pl.ds(0, cap)], tlo[:, pl.ds(0, cap)]
-        both_parts = dot_nn(jnp.concatenate([high, low], axis=0), xy_high)
-        part = both_parts[: 3 * tall_z] + both_parts[3 * tall_z :] + dot_nn(high, xy_low)
+        part = halved(lambda a, b: (high[a:b], low[a:b]), xy_high, xy_low, dot_nn)
         heights = tz[:, pl.ds(0, cap)]
         return jnp.concatenate(
             [
@@ -408,8 +427,13 @@
         low_row, high_row = reach(xi)
         row, count = pl.ds(low_row, high_row - low_row), (last - first) * cap
         at, here = pl.ds(first * cap, count), pl.ds((xi * near_y + yi) * cap, count)
+        half = 3 * tall_z
+        if high_row - low_row < wide_xy:
+            tables = jnp.concatenate([thi[row, at], tlo[row, at]], axis=0)
+            both_parts = dot_nt(wide[:, here], tables)
+            both_parts = both_parts[:half] + both_parts[half:]
+            return both_parts[:, : high_row - low_row] + both_parts[:, high_row - low_row :]
         both_parts = dot_nt(wide[:, here], thi[row, at])
-        half = 3 * tall_z
         return both_parts[:half] + both_parts[half:] + dot_nt(wide[pl.ds(0, half), here], tlo[row, at])
 
     def spread(turn, vector):
@@ -423,22 +447,29 @@
         for c in range(3):
             grid[c] = own[c * tall_z : (c + 1) * tall_z]
         spread_edges(turn, 0)
-        wait_round(turn, 1)
+        spread_sides(turn, 1)
+        wait_round(turn, 2)
+        spread_edges(turn, *range(1, near_x))
+
+    def spread_sides(turn, part):
+        wait_round(turn, part)
         for xi in range(1, near_x):
-            first = middle + (xi - 1) * near_y
-            for number in range(first, first + near_y):
-                fill(number, [taken(turn, number, c) for c in range(3)])
-            low_row, high_row = reach(xi)
-            side = contract(first, first + near_y)
-            for c in range(3):
-                grid[c, :, pl.ds(low_row, high_row - low_row)] += side[c * tall_z : (c + 1) * tall_z]
-        wait_round(turn, 2)
-        for xi in range(1, near_x):
-            spread_edges(turn, xi)
-
-    def spread_edges(turn, xi):
-        if each:
-            low_row, high_row = reach(xi)
+            numbers = [number for number in range(*parts[part]) if places[number][0] == xi]
+            if numbers:
+                for number in numbers:
+                    fill(number, [taken(turn, number, c) for c in range(3)])
+                low_row, high_row = reach(xi)
+                side = contract(numbers[0], numbers[-1] + 1)
+                for c in range(3):
+                    grid[c, :, pl.ds(low_row, high_row - low_row)] += side[c * tall_z : (c + 1) * tall_z]
+
+    def spread_edges(turn, *near):
+        if not each or not near:
+            return
+        total = jnp.zeros((wide_xy, 48), jnp.float32)
+        for xi in near:
+            start, planes = span(groups[0][xi][1], size_x)
+            low_row, high_row = start * rows_y, round_up((start + planes) * rows_y + HIGH, 16)
             row = pl.ds(low_row, high_row - low_row)
             begin = edges[xi * each]
             rows = [[], [], []]
@@ -450,16 +481,20 @@
             rounded = value.astype(jnp.bfloat16).astype(jnp.float32)
             both_parts = jnp.concatenate([rounded, value - rounded], axis=0).astype(jnp.bfloat16)
             at = pl.ds(begin * cap, each * cap)
-            part = dot_nt(both_parts, thi[row, at]) + dot_nt(both_parts, tlo[row, at])
-            part = part[:24] + part[24:]
-            which = wide_line[:, : high_row - low_row]
-            for c in range(3):
-                edge = part[c * 8 : c * 8 + 8]
-                early, late = pltpu.roll(edge, 6, 0), pltpu.roll(edge, 3, 0)
-                grid[c, pl.ds(0, 8), row] += jnp.where(which >= 6, early, 0.0)
-                grid[c, pl.ds(low_z, 8), row] += jnp.where(which < 2, early, 0.0)
-                grid[c, pl.ds(size_z, 8), row] += jnp.where(which == 7, late, 0.0)
-                grid[c, pl.ds(low_z + size_z, 8), row] += jnp.where(which < 3, late, 0.0)
+            part = dot_nt(jnp.concatenate([thi[row, at], tlo[row, at]], axis=0), both_parts)
+            part = part[: high_row - low_row] + part[high_row - low_row :]
+            pieces = [jnp.zeros((low_row, 48), jnp.float32)] * (low_row > 0) + [part]
+            pieces += [jnp.zeros((wide_xy - high_row, 48), jnp.float32)] * (high_row < wide_xy)
+            total = total + jnp.concatenate(pieces, axis=0)
+        turned = jnp.transpose(jnp.concatenate([total, jnp.zeros((wide_xy, 80), jnp.float32)], axis=1))
+        turned = turned[:24] + turned[24:48]
+        for c in range(3):
+            edge = turned[c * 8 : c * 8 + 8]
+            early, late = pltpu.roll(edge, 6, 0), pltpu.roll(edge, 3, 0)
+            grid[c, pl.ds(0, 8)] += jnp.where(wide_line >= 6, early, 0.0)
+            grid[c, pl.ds(low_z, 8)] += jnp.where(wide_line < 2, early, 0.0)
+            grid[c, pl.ds(size_z, 8)] += jnp.where(wide_line == 7, late, 0.0)
+            grid[c, pl.ds(low_z + size_z, 8)] += jnp.where(wide_line < 3, late, 0.0)
 
     def slide(value, step):
         return pltpu.roll(value, (-step) % wide_xy, 1)
@@ -528,18 +563,16 @@
         copy.start()
     build(0)
     drain(slabs, srecv.at[0])
-    for copy in halos[0]:
-        copy.wait_recv()
+    drain(ghosts[8], ghosts[10].at[0])
     assemble(0)
     residual = live * (target[...] - interpolate(planar[pl.ds(0, 3)].reshape(3 * tall_z, wide_xy)))
     put(1, residual)
     send_round(1)
-    for part in range(3):
+    for part in range(STAGES):
         wait_round(0, part)
-    for number in range(1, len(slots)):
-        build(number)
-    for copy in halos[1]:
-        copy.wait_recv()
+        for number in range(*parts[part]):
+            build(number)
+    drain(ghosts[19], ghosts[21].at[0])
     assemble(1)
 
     image = apply(1, residual)
@@ -547,10 +580,10 @@
     answer = None
     norm_before = alpha = None
     for step in range(ITERS):
-        sums = partial_sums(residual, image)
         if step + 1 < ITERS:
             put(step + 2, image)
             send_round(step + 2)
+        sums = partial_sums(residual, image)
         if direct:
             send_directly(step, sums)
             if step + 1 < ITERS:
@@ -581,8 +614,10 @@
             residual = residual - alpha * along
             image = image - alpha * along_image
     out[...] = answer
-    for copy in halos[0] + halos[1] + sent:
+    for copy in sent:
         copy.wait_send()
+    drain(ghosts[8], ghosts[9].at[0])
+    drain(ghosts[19], ghosts[20].at[0])
     drain(slabs, ssend.at[0])
     if len(slots) > 1:
         at = pl.ds(1, len(slots) - 1)
@@ -592,15 +627,16 @@
         drain(dbuf.at[:, pl.ds(1, len(everyone))], dsend.at[0])
 
 
-def ghost_scratch(sizes, names, low, high):
+def ghost_scratch(sizes, beside, names, low, high):
     size_x, size_y, size_z = sizes
     fields, kinds = len(names), len(names) * (low + high)
     shapes = [
         (fields, low, size_y, size_z), (fields, high, size_y, size_z),
         (kinds, size_x, size_z), (kinds * low, size_z), (kinds * high, size_z),
-        (2, kinds, size_x, size_z), (2, kinds * low, size_z), (2, kinds * high, size_z),
+        (beside, kinds, size_x, size_z), (beside, kinds * low, size_z), (beside, kinds * high, size_z),
+        (fields * (low + high) * size_y + beside * kinds * (size_x + low + high), size_z),
     ]
-    return [pltpu.VMEM(shape, jnp.float32) for shape in shapes] + [pltpu.SemaphoreType.DMA((8,))] * 2
+    return [pltpu.VMEM(shape, jnp.float32) for shape in shapes] + [pltpu.SemaphoreType.DMA((1,))] * 2
 
 
 def body(mesh_counts, density, base_velocity, cells, offsets, target, stiffness, counts):
@@ -644,14 +680,14 @@
             pltpu.VMEM((3, tall_z, wide_xy), jnp.float32),
             pltpu.SemaphoreType.DMA((7,)),
             pltpu.SemaphoreType.DMA((2,)),
-            pltpu.SemaphoreType.DMA((turns, 3)),
+            pltpu.SemaphoreType.DMA((turns, STAGES)),
             pltpu.SemaphoreType.DMA((ITERS, 3, longest - 1) if most == 1 else (1, 1, 1)),
             pltpu.SemaphoreType.DMA((ITERS, 3, longest - 1) if most == 1 else (1, 1, 1)),
             pltpu.SemaphoreType.DMA((1,)),
             pltpu.SemaphoreType.DMA((ITERS,)),
             pltpu.SemaphoreType.DMA((1,)),
             pltpu.SemaphoreType.DMA((1,)),
-        ] + [item for group in GHOSTS for item in ghost_scratch(sizes, *group)],
+        ] + [item for group in GHOSTS for item in ghost_scratch(sizes, len({1 % mesh_counts[1], (-1) % mesh_counts[1]}), *group)],
         compiler_params=pltpu.CompilerParams(
             collective_id=0, has_side_effects=True, vmem_limit_bytes=60 * 1024 * 1024
         ),

time: 37.9 us -> 37 us (0.976)
  Pallas kernels: 36.5 us -> 35.6 us
    pallas_call x1, Pallas kernels: 36.5 us -> 35.6 us  [body(): pl.pallas_call(functools.partial(kernel, mesh_counts, sizes), out_shape=p...]
where the time goes in v5:
time: 37 us; the launch traced here: 36.9 us
  Pallas kernels  35.6 us (96%)
  between operations  0.66 us (2%)
  local copies, waits for them, and re-layouts  0.6 us (2%)
    pallas_call x1, Pallas kernels, body(): pl.pallas_call(functools.partial(kernel, mesh_counts, sizes), out_shape=p...  35.6 us

profile of v5, /device:TPU:0, one launch (start us, length us, event | category | flops | bytes accessed | tf_op | source)
XLA Modules:
  0.0 36.9 jit_solution(16804993560738208605)
XLA Ops:
  0.7 35.6 %shard_map.73 = f32[3,256]{1,0:T(4,128)S(1)} custom-call(f32[8,8,128]{2,1,0:T(8,128)} %density_in.1, f32[3,8,8,128]{3,2,1,0:T(8,128)} %velocity_in.1, s32[3,256]{1,0:T(4,128)} %cells_in.1, f32[3,256]{1,0:T(4,128)} %offsets_in.1, f32[3,256]{1,0:T(4,128)} %target_in.1, f32[1,256]{1,0:T(1,128)} %bitcast.1, s32[1]{0:T(128)S(6)} %copy.10.live_in), custom_call_target="tpu_custom_call" | custom-call | tf_op jit(solution)/shard_map/pallas_call | solution.py:655
  36.3 0.6 %copy.9 = f32[3,256]{1,0:T(4,128)} copy(f32[3,256]{1,0:T(4,128)S(1)} %shard_map.73) | data formatting | bytes 6144

commit v6 on v5

--- a/solution.py
+++ b/solution.py
@@ -185,32 +185,10 @@
             turned = jnp.transpose(level)
             slab[pair] = jnp.where(line[:, : rows_y * size_x] < HIGH, turned[:8], turned[size_z - 8 :])
 
-    def assemble(number):
-        (names, low, high), (xl, xh, pack, lpack, hpack, yb, lb, hb, tally, send, recv) = GHOSTS[number], ghosts[11 * number : 11 * number + 11]
-        kinds = low + high
-        k_below, k_above = offs_y.index((-1) % counts[1]), offs_y.index(1 % counts[1])
-        empty = jnp.zeros((8, size_z), jnp.float32)
-
-        def core(f, p):
-            if p < LOW:
-                return xl[f, p - LOW + low] if p >= LOW - low else empty
-            if p < LOW + size_x:
-                return block[names[f], p - LOW]
-            return xh[f, p - LOW - size_x] if p < LOW + size_x + high else empty
-
-        def beside(f, p, j):
-            k, kind = (k_below if j < low else k_above), f * kinds + j
-            if LOW - low <= p < LOW:
-                return lb[k, pl.ds(kind * low + p - LOW + low, 1), :]
-            if LOW <= p < LOW + size_x:
-                return yb[k, kind, pl.ds(p - LOW, 1), :]
-            if LOW + size_x <= p < LOW + size_x + high:
-                return hb[k, pl.ds(kind * high + p - LOW - size_x, 1), :]
-            return None
-
+    def ends_of(number):
+        names = GHOSTS[number][0]
         lane = lax.broadcasted_iota(jnp.int32, (8, wide_xy), 1) - (8 - LOW)
         plane, level = lane // rows_y, lane % rows_y
-        blank = jnp.zeros((wide_xy - (wide_x + 1) * rows_y, size_z), jnp.float32)
         ends = {}
         for shift_x, shift_y in itertools.product((0, -1, 1), (0, -1, 1)):
             inside = (lane >= 0) & (plane < wide_x) & (level < size_y + LOW + HIGH)
@@ -224,6 +202,35 @@
                     edge = jnp.concatenate([got[name // 2], jnp.zeros((8, wide_xy - rows_y * size_x), jnp.float32)], axis=1)
                     edge = pltpu.roll(edge, by % wide_xy, 1)
                     ends[name, shift_z] = jnp.where(inside, edge, ends.get((name, shift_z), 0.0))
+        return [
+            (jnp.where(wide_line >= 8 - LOW, ends[name, -1], 0.0), jnp.where(wide_line < HIGH, ends[name, 1], 0.0))
+            for name in names
+        ]
+
+    def assemble(number, ends):
+        (names, low, high), (xl, xh, pack, lpack, hpack, yb, lb, hb, tally, send, recv) = GHOSTS[number], ghosts[11 * number : 11 * number + 11]
+        kinds = low + high
+        k_below, k_above = offs_y.index((-1) % counts[1]), offs_y.index(1 % counts[1])
+        empty = jnp.zeros((8, size_z), jnp.float32)
+
+        def core(f, p):
+            if p < LOW:
+                return xl[f, p - LOW + low] if p >= LOW - low else empty
+            if p < LOW + size_x:
+                return block[names[f], p - LOW]
+            return xh[f, p - LOW - size_x] if p < LOW + size_x + high else empty
+
+        def beside(f, p, j):
+            k, kind = (k_below if j < low else k_above), f * kinds + j
+            if LOW - low <= p < LOW:
+                return lb[k, pl.ds(kind * low + p - LOW + low, 1), :]
+            if LOW <= p < LOW + size_x:
+                return yb[k, kind, pl.ds(p - LOW, 1), :]
+            if LOW + size_x <= p < LOW + size_x + high:
+                return hb[k, pl.ds(kind * high + p - LOW - size_x, 1), :]
+            return None
+
+        blank = jnp.zeros((wide_xy - (wide_x + 1) * rows_y, size_z), jnp.float32)
         for f, name in enumerate(names):
             tiles = []
             for p in range(wide_x + 1):
@@ -234,8 +241,8 @@
                         ghost = jnp.where(line == (8 - low + j if j < low else j - low), row, ghost)
                 tiles += [ghost, core(f, p) if p < wide_x else empty]
             planar[name, pl.ds(low_z, size_z)] = jnp.transpose(jnp.concatenate(tiles + [blank], axis=0))
-            planar[name, pl.ds(0, 8)] = jnp.where(wide_line >= 8 - LOW, ends[name, -1], 0.0)
-            planar[name, pl.ds(low_z + size_z, 8)] = jnp.where(wide_line < HIGH, ends[name, 1], 0.0)
+            planar[name, pl.ds(0, 8)] = ends[f][0] if ends else jnp.zeros((8, wide_xy), jnp.float32)
+            planar[name, pl.ds(low_z + size_z, 8)] = ends[f][1] if ends else jnp.zeros((8, wide_xy), jnp.float32)
 
     loads = [
         pltpu.make_async_copy(source, target_ref, lsem.at[number])
@@ -413,6 +420,17 @@
             axis=0,
         )
 
+    def interpolate_ends(field):
+        high, low = split(field)
+        xy_high, xy_low = thi[:, pl.ds(0, cap)], tlo[:, pl.ds(0, cap)]
+        both_parts = jnp.concatenate([high, low], axis=0)
+        part = dot_nn(both_parts, xy_high) + dot_nn(both_parts, xy_low)
+        part = part[:48] + part[48:]
+        heights = jnp.concatenate([tz[pl.ds(0, 8), pl.ds(0, cap)], tz[pl.ds(low_z + size_z, 8), pl.ds(0, cap)]], axis=0)
+        return jnp.concatenate(
+            [jnp.sum(part[16 * c : 16 * c + 16] * heights, axis=0, keepdims=True) for c in range(3)], axis=0
+        )
+
     def fill(number, rows):
         xi, yi, _ = places[number]
         at = pl.ds((xi * near_y + yi) * cap, cap)
@@ -562,10 +580,12 @@
     for copy in halos[1]:
         copy.start()
     build(0)
+    drain(ghosts[8], ghosts[10].at[0])
+    assemble(0, None)
+    inner = interpolate(planar[pl.ds(0, 3)].reshape(3 * tall_z, wide_xy))
     drain(slabs, srecv.at[0])
-    drain(ghosts[8], ghosts[10].at[0])
-    assemble(0)
-    residual = live * (target[...] - interpolate(planar[pl.ds(0, 3)].reshape(3 * tall_z, wide_xy)))
+    outer = interpolate_ends(jnp.concatenate([end for pair in ends_of(0) for end in pair], axis=0))
+    residual = live * (target[...] - (inner + outer))
     put(1, residual)
     send_round(1)
     for part in range(STAGES):
@@ -573,7 +593,7 @@
         for number in range(*parts[part]):
             build(number)
     drain(ghosts[19], ghosts[21].at[0])
-    assemble(1)
+    assemble(1, ends_of(1))
 
     image = apply(1, residual)
     direction, along, along_image = residual, image, None

time: 37 us -> 36.7 us (level)
  no operation moved by 1% of the time
where the time goes in v6:
time: 36.7 us; the launch traced here: 36.5 us
  Pallas kernels  35.3 us (96%)
  between operations  0.66 us (2%)
  local copies, waits for them, and re-layouts  0.6 us (2%)
    pallas_call x1, Pallas kernels, body(): pl.pallas_call(functools.partial(kernel, mesh_counts, sizes), out_shape=p...  35.3 us

profile of v6, /device:TPU:0, one launch (start us, length us, event | category | flops | bytes accessed | tf_op | source)
XLA Modules:
  0.0 36.5 jit_solution(17095394697896048755)
XLA Ops:
  0.7 35.3 %shard_map.73 = f32[3,256]{1,0:T(4,128)S(1)} custom-call(f32[8,8,128]{2,1,0:T(8,128)} %density_in.1, f32[3,8,8,128]{3,2,1,0:T(8,128)} %velocity_in.1, s32[3,256]{1,0:T(4,128)} %cells_in.1, f32[3,256]{1,0:T(4,128)} %offsets_in.1, f32[3,256]{1,0:T(4,128)} %target_in.1, f32[1,256]{1,0:T(1,128)} %bitcast.1, s32[1]{0:T(128)S(6)} %copy.10.live_in), custom_call_target="tpu_custom_call" | custom-call | tf_op jit(solution)/shard_map/pallas_call | solution.py:675
  36.0 0.6 %copy.9 = f32[3,256]{1,0:T(4,128)} copy(f32[3,256]{1,0:T(4,128)S(1)} %shard_map.73) | data formatting | bytes 6144
